TPU v7x, 32 devices: a whole 2x2x4 slice. The times are simulated.
32 devices in a mesh: grp: 2 (over x), comp: 4 (over z), row: 4 (over y, core).
Axes of the slice: x: 2, y: 2, z: 4, core: 2. Of those that a mesh axis runs over, the one named last changes fastest.
Arguments:
- points: bfloat16 [8192, 512], P(('grp', 'row')), parts along dimension 0
- mu_init: float32 [2, 8192, 256], P(None, ('grp', 'comp')), parts along dimension 1
- logpi_init: float32 [2, 8192], P(None, ('grp', 'comp')), parts along dimension 1
- inv_temp: float32 [3], replicated
Outputs:
- output 1: float32 [2, 8192, 256], P(None, ('grp', 'comp')), parts along dimension 1
- output 2: float32 [2, 8192], P(None, ('grp', 'comp')), parts along dimension 1
- output 3: float32 [2, 8192], P(None, ('grp', 'row')), parts along dimension 1
There are 2 independent parts. A program takes and returns all parts, laid end to end along the dimension named above; an argument that names none is the same for every part.
All inputs are finite; a program needn't handle non-finite values.
Results may differ from a plain program's by a relative error of at most 0.00106792.
Values are sent between devices in bfloat16 or wider.
A program may use at most 1 GiB of HBM per device.

v0:
```python
import jax
import jax.numpy as jnp
from jax import lax
from jax.sharding import PartitionSpec as P

EPS_COUNT = 1e-6
PRIOR_ALPHA = 1e-3


def solution(mesh):
    comp_size = mesh.shape["comp"]
    row_size = mesh.shape["row"]

    def local_fit(x_local, mu_init, logpi_init, inv_temp):
        n_rows, full_dim = x_local.shape
        half_dim = full_dim // 2
        n_local = mu_init.shape[1]
        total_pts = n_rows * row_size
        total_comp = n_local * comp_size
        x_fits = jnp.transpose(x_local.reshape(n_rows, 2, half_dim), (1, 0, 2))
        sq_norm = jnp.sum(jnp.square(x_fits.astype(jnp.float32)), axis=2)
        mean_vecs = mu_init
        log_wts = logpi_init
        for sweep_idx in range(inv_temp.shape[0]):
            beta_t = inv_temp[sweep_idx]
            mu_sq = jnp.sum(mean_vecs * mean_vecs, axis=2)
            cross_dot = jnp.einsum("snh,skh->snk", x_fits, mean_vecs.astype(jnp.bfloat16), preferred_element_type=jnp.float32)
            logits = log_wts[:, None, :] - beta_t * (sq_norm[:, :, None] - 2.0 * cross_dot + mu_sq[:, None, :])
            row_max = lax.pmax(jnp.max(logits, axis=2), "comp")
            shifted = jnp.exp(logits - row_max[:, :, None])
            row_sum = lax.psum(jnp.sum(shifted, axis=2), "comp")
            log_norm = row_max + jnp.log(row_sum)
            resp_f = shifted / row_sum[:, :, None]
            counts = jnp.sum(resp_f, axis=1)
            stat_sum = jnp.einsum("snk,snh->skh", resp_f.astype(jnp.bfloat16), x_fits, preferred_element_type=jnp.float32)
            counts, stat_sum = lax.psum((counts, stat_sum), "row")
            mean_vecs = stat_sum / (counts[:, :, None] + EPS_COUNT)
            log_wts = jnp.log((counts + PRIOR_ALPHA) / (total_pts + total_comp * PRIOR_ALPHA))
        return mean_vecs, log_wts, log_norm

    return jax.shard_map(
        local_fit,
        mesh=mesh,
        in_specs=(P(("grp", "row"), None), P(None, ("grp", "comp"), None), P(None, ("grp", "comp")), P()),
        out_specs=(P(None, ("grp", "comp"), None), P(None, ("grp", "comp")), P(None, ("grp", "row"))),
        check_vma=False,
    )
```

profile of v0, /device:TPU:0, one launch (start us, length us, event | category | flops | bytes accessed | tf_op | source)
XLA Modules:
  0.0 301.1 jit_solution(12132038897971969081)
XLA Ops:
  7.2 0.0 all-reduce.4.cloned.1.call-start
  7.2 1.4 fusion.33
  8.6 2.5 multiply_reduce_fusion.2
  11.1 0.0 copy-start.1
  11.1 0.0 copy-start
  11.1 7.7 %fusion.14 = (f32[2,1024]{1,0:T(2,128)S(1)}, f32[2,1024,1024]{1,2,0:T(8,128)}) fusion(f32[2,1024]{1,0:T(2,128)S(1)} %get-tuple-element.18, f32[2,1024]{1,0:T(2,128)S(1)} %get-tuple-element.19, f32[]{:T(128)} %bitcast, f32[2,1024]{1,0:T(2,128)} %param.6, f32[2,1024,256]{2,1,0:T(8,128)} %param.5, bf16[128,2,8,256]{3,2,1,0:T(8,128)(2,1)} %bitcast.65), kind=kOutput, calls=%fused_computation.22 | convolution fusion | flops 1086846976 | bytes 11567108 | tf_op jit(solution)/shard_map/snh,skh->snk/dot_general | solution.py:27
  18.8 13.7 %pmax.21 = f32[2,1024]{1,0:T(2,128)S(1)} all-reduce(f32[2,1024]{1,0:T(2,128)S(1)} %get-tuple-element.12), channel_id=1, replica_groups=mesh['grp'=2,'comp'=4,'row'=4] {'comp'}, use_global_device_ids=true, to_apply=%region_3.0 | all-reduce | flops 2048 | bytes 16384 | tf_op jit(solution)/shard_map/pmax | solution.py:29
  32.5 0.0 copy-done.1
  32.5 5.4 %fusion.3 = f32[2,1024]{1,0:T(2,128)S(1)} fusion(f32[2,1024]{1,0:T(2,128)S(1)} %pmax.21, f32[2,1024]{1,0:T(2,128)S(1)} %get-tuple-element.18, f32[2,1024,1024]{1,2,0:T(8,128)} %get-tuple-element.13, f32[2,1024]{1,0:T(2,128)S(1)} %get-tuple-element.19, f32[]{:T(128)} %bitcast, f32[2,1024]{1,0:T(2,128)S(1)} %copy-done.1), kind=kLoop, calls=%fused_computation.11 | loop fusion | flops 14678016 | bytes 8429572 | tf_op jit(solution)/shard_map/reduce_sum | solution.py:31
  38.0 8.5 %psum.63 = f32[2,1024]{1,0:T(2,128)S(1)} all-reduce(f32[2,1024]{1,0:T(2,128)S(1)} %fusion.3), channel_id=1, replica_groups=mesh['grp'=2,'comp'=4,'row'=4] {'comp'}, use_global_device_ids=true, to_apply=%region_5.0 | all-reduce | flops 2048 | bytes 16384 | tf_op jit(solution)/shard_map/psum | solution.py:31
  46.5 0.0 copy-done
  46.5 6.9 %fusion.12 = f32[2,1024,256]{2,1,0:T(8,128)} fusion(bf16[128,2,8,256]{3,2,1,0:T(8,128)(2,1)S(1)} %bitcast.66, f32[2,1024]{1,0:T(2,128)S(1)} %psum.63, f32[2,1024]{1,0:T(2,128)S(1)} %pmax.21, f32[2,1024]{1,0:T(2,128)S(1)} %get-tuple-element.18, f32[2,1024,1024]{1,2,0:T(8,128)} %get-tuple-element.13, f32[2,1024]{1,0:T(2,128)S(1)} %get-tuple-element.19, ...), kind=kOutput, calls=%fused_computation.20 | convolution fusion | flops 1090519040 | bytes 11575300 | tf_op jit(solution)/shard_map/snk,snh->skh/dot_general | solution.py:35
  53.4 0.0 all-reduce.4.cloned.1.call-update
  53.4 0.0 all-reduce.6.cloned.1.call-start
  53.5 6.1 %fusion.32 = f32[2,1024]{1,0:T(2,128)S(1)} fusion(f32[2,1024]{1,0:T(2,128)S(1)} %psum.63, f32[2,1024]{1,0:T(2,128)S(1)} %pmax.21, f32[2,1024]{1,0:T(2,128)S(1)} %get-tuple-element.18, f32[2,1024,1024]{1,2,0:T(8,128)} %get-tuple-element.13, f32[2,1024]{1,0:T(2,128)S(1)} %get-tuple-element.19, f32[]{:T(128)} %bitcast, f32[2,1024]{1,0:T(2,128)S(1)} %copy-done.1), kind=kLoop, calls=%fused_computation.52 | loop fusion | flops 16775168 | bytes 8437764 | tf_op jit(solution)/shard_map/reduce_sum | solution.py:34
  59.6 6.5 %psum.64 = f32[2,1024]{1,0:T(2,128)S(1)} all-reduce(f32[2,1024]{1,0:T(2,128)S(1)} %fusion.32), channel_id=1, replica_groups=mesh['grp'=2,'comp'=4,'row'=4] {'row'}, use_global_device_ids=true, to_apply=%region_7.0 | all-reduce | flops 2048 | bytes 16384 | tf_op jit(solution)/shard_map/psum | solution.py:36
  66.2 38.6 %all-reduce.4.cloned.1.call-done = f32[2,1024,256]{2,1,0:T(8,128)} async-done(((f32[2,1024,256]{2,1,0:T(8,128)}), f32[2,1024,256]{2,1,0:T(8,128)}) %all-reduce.4.cloned.1.call-update) | async-done | bytes 2097168 | tf_op jit(solution)/shard_map/psum | solution.py:36
  104.7 2.2 multiply_reduce_fusion.1
  107.0 6.4 %bitcast_reduce_fusion.1 = (f32[2,1024]{1,0:T(2,128)S(1)}, f32[2,1024,1024]{1,2,0:T(8,128)}) fusion(f32[2,1024]{1,0:T(2,128)S(1)} %multiply_reduce_fusion.1, f32[2,1024]{1,0:T(2,128)S(1)} %get-tuple-element.19, f32[]{:T(128)} %bitcast.2, f32[2,1024]{1,0:T(2,128)S(1)} %get-tuple-element.7, bf16[128,2,8,256]{3,2,1,0:T(8,128)(2,1)S(1)} %bitcast.67, ...), kind=kOutput, calls=%fused_computation.4 | convolution fusion | flops 1087371264 | bytes 11575300 | tf_op jit(solution)/shard_map/snh,skh->snk/dot_general | solution.py:27
  113.4 11.8 %pmax.22 = f32[2,1024]{1,0:T(2,128)S(1)} all-reduce(f32[2,1024]{1,0:T(2,128)S(1)} %get-tuple-element.14), channel_id=1, replica_groups=mesh['grp'=2,'comp'=4,'row'=4] {'comp'}, use_global_device_ids=true, to_apply=%region_11.0 | all-reduce | flops 2048 | bytes 16384 | tf_op jit(solution)/shard_map/pmax | solution.py:29
  125.2 5.9 %fusion.5 = f32[2,1024]{1,0:T(2,128)S(1)} fusion(f32[2,1024]{1,0:T(2,128)S(1)} %pmax.22, f32[2,1024]{1,0:T(2,128)S(1)} %multiply_reduce_fusion.1, f32[2,1024,1024]{1,2,0:T(8,128)} %get-tuple-element.15, f32[2,1024]{1,0:T(2,128)S(1)} %get-tuple-element.19, f32[]{:T(128)} %bitcast.2, f32[2,1024]{1,0:T(2,128)S(1)} %get-tuple-element.7), kind=kLoop, calls=%fused_computation.13 | loop fusion | flops 14678016 | bytes 8429572 | tf_op jit(solution)/shard_map/reduce_sum | solution.py:31
  131.1 8.7 %psum.66 = f32[2,1024]{1,0:T(2,128)S(1)} all-reduce(f32[2,1024]{1,0:T(2,128)S(1)} %fusion.5), channel_id=1, replica_groups=mesh['grp'=2,'comp'=4,'row'=4] {'comp'}, use_global_device_ids=true, to_apply=%region_13.0 | all-reduce | flops 2048 | bytes 16384 | tf_op jit(solution)/shard_map/psum | solution.py:31
  139.8 7.9 %fusion.10 = f32[2,1024,256]{2,1,0:T(8,128)} fusion(bf16[128,2,8,256]{3,2,1,0:T(8,128)(2,1)S(1)} %bitcast.68, f32[2,1024]{1,0:T(2,128)S(1)} %psum.66, f32[2,1024]{1,0:T(2,128)S(1)} %pmax.22, f32[2,1024]{1,0:T(2,128)S(1)} %multiply_reduce_fusion.1, f32[2,1024,1024]{1,2,0:T(8,128)} %get-tuple-element.15, f32[2,1024]{1,0:T(2,128)S(1)} %get-tuple-element.19, ...), kind=kOutput, calls=%fused_computation.18 | convolution fusion | flops 1090519040 | bytes 11575300 | tf_op jit(solution)/shard_map/snk,snh->skh/dot_general | solution.py:35
  147.7 0.0 all-reduce.6.cloned.1.call-update
  147.7 0.0 all-reduce.8.cloned.1.call-start
  147.8 5.8 %fusion.30 = f32[2,1024]{1,0:T(2,128)S(1)} fusion(f32[2,1024]{1,0:T(2,128)S(1)} %psum.66, f32[2,1024]{1,0:T(2,128)S(1)} %pmax.22, f32[2,1024]{1,0:T(2,128)S(1)} %multiply_reduce_fusion.1, f32[2,1024,1024]{1,2,0:T(8,128)} %get-tuple-element.15, f32[2,1024]{1,0:T(2,128)S(1)} %get-tuple-element.19, f32[]{:T(128)} %bitcast.2, f32[2,1024]{1,0:T(2,128)S(1)} %get-tuple-element.7), kind=kLoop, calls=%fused_computation.51 | loop fusion | flops 16775168 | bytes 8437764 | tf_op jit(solution)/shard_map/reduce_sum | solution.py:34
  153.6 6.6 %psum.67 = f32[2,1024]{1,0:T(2,128)S(1)} all-reduce(f32[2,1024]{1,0:T(2,128)S(1)} %fusion.30), channel_id=1, replica_groups=mesh['grp'=2,'comp'=4,'row'=4] {'row'}, use_global_device_ids=true, to_apply=%region_15.0 | all-reduce | flops 2048 | bytes 16384 | tf_op jit(solution)/shard_map/psum | solution.py:36
  160.2 38.0 %all-reduce.6.cloned.1.call-done = f32[2,1024,256]{2,1,0:T(8,128)} async-done(((f32[2,1024,256]{2,1,0:T(8,128)}), f32[2,1024,256]{2,1,0:T(8,128)}) %all-reduce.6.cloned.1.call-update) | async-done | bytes 2097168 | tf_op jit(solution)/shard_map/psum | solution.py:36
  198.2 2.2 multiply_reduce_fusion
  200.4 6.4 %bitcast_reduce_fusion = (f32[2,1024]{1,0:T(2,128)S(1)}, f32[2,1024,1024]{1,2,0:T(8,128)}) fusion(f32[2,1024]{1,0:T(2,128)S(1)} %multiply_reduce_fusion, f32[2,1024]{1,0:T(2,128)S(1)} %get-tuple-element.19, f32[]{:T(128)} %bitcast.4, f32[2,1024]{1,0:T(2,128)S(1)} %get-tuple-element.5, bf16[128,2,8,256]{3,2,1,0:T(8,128)(2,1)S(1)} %bitcast.69, ...), kind=kOutput, calls=%fused_computation.1 | convolution fusion | flops 1087371264 | bytes 11575300 | tf_op jit(solution)/shard_map/snh,skh->snk/dot_general | solution.py:27
  206.8 11.8 %pmax.23 = f32[2,1024]{1,0:T(2,128)S(1)} all-reduce(f32[2,1024]{1,0:T(2,128)S(1)} %get-tuple-element.16), channel_id=1, replica_groups=mesh['grp'=2,'comp'=4,'row'=4] {'comp'}, use_global_device_ids=true, to_apply=%region_19.0 | all-reduce | flops 2048 | bytes 16384 | tf_op jit(solution)/shard_map/pmax | solution.py:29
  218.6 5.9 %fusion.7 = f32[2,1024]{1,0:T(2,128)S(1)} fusion(f32[2,1024]{1,0:T(2,128)S(1)} %pmax.23, f32[2,1024]{1,0:T(2,128)S(1)} %multiply_reduce_fusion, f32[2,1024,1024]{1,2,0:T(8,128)} %get-tuple-element.17, f32[2,1024]{1,0:T(2,128)S(1)} %get-tuple-element.19, f32[]{:T(128)} %bitcast.4, f32[2,1024]{1,0:T(2,128)S(1)} %get-tuple-element.5), kind=kLoop, calls=%fused_computation.15 | loop fusion | flops 14678016 | bytes 8429572 | tf_op jit(solution)/shard_map/reduce_sum | solution.py:31
  224.5 8.5 %psum.69 = f32[2,1024]{1,0:T(2,128)S(1)} all-reduce(f32[2,1024]{1,0:T(2,128)S(1)} %fusion.7), channel_id=1, replica_groups=mesh['grp'=2,'comp'=4,'row'=4] {'comp'}, use_global_device_ids=true, to_apply=%region_21.0 | all-reduce | flops 2048 | bytes 16384 | tf_op jit(solution)/shard_map/psum | solution.py:31
  233.0 7.8 %fusion.8 = f32[2,1024,256]{2,1,0:T(8,128)} fusion(bf16[128,2,8,256]{3,2,1,0:T(8,128)(2,1)S(1)} %bitcast.70, f32[2,1024]{1,0:T(2,128)S(1)} %psum.69, f32[2,1024]{1,0:T(2,128)S(1)} %pmax.23, f32[2,1024]{1,0:T(2,128)S(1)} %multiply_reduce_fusion, f32[2,1024,1024]{1,2,0:T(8,128)} %get-tuple-element.17, f32[2,1024]{1,0:T(2,128)S(1)} %get-tuple-element.19, ...), kind=kOutput, calls=%fused_computation.16 | convolution fusion | flops 1090519040 | bytes 11575300 | tf_op jit(solution)/shard_map/snk,snh->skh/dot_general | solution.py:35
  240.9 0.0 all-reduce.8.cloned.1.call-update
  240.9 5.8 %fusion.27 = f32[2,1024]{1,0:T(2,128)S(1)} fusion(f32[2,1024]{1,0:T(2,128)S(1)} %psum.69, f32[2,1024]{1,0:T(2,128)S(1)} %pmax.23, f32[2,1024]{1,0:T(2,128)S(1)} %multiply_reduce_fusion, f32[2,1024,1024]{1,2,0:T(8,128)} %get-tuple-element.17, f32[2,1024]{1,0:T(2,128)S(1)} %get-tuple-element.19, f32[]{:T(128)} %bitcast.4, f32[2,1024]{1,0:T(2,128)S(1)} %get-tuple-element.5), kind=kLoop, calls=%fused_computation.50 | loop fusion | flops 16775168 | bytes 8437764 | tf_op jit(solution)/shard_map/reduce_sum | solution.py:34
  246.7 6.6 %psum.71 = f32[2,1024]{1,0:T(2,128)S(1)} all-reduce(f32[2,1024]{1,0:T(2,128)S(1)} %fusion.27), channel_id=1, replica_groups=mesh['grp'=2,'comp'=4,'row'=4] {'row'}, use_global_device_ids=true, to_apply=%region_24.0 | all-reduce | flops 2048 | bytes 16384 | tf_op jit(solution)/shard_map/psum | solution.py:36
  253.3 0.6 log_add_fusion
  253.9 0.6 multiply_log_fusion
  254.5 36.8 %all-reduce.8.cloned.1.call-done = f32[2,1024,256]{2,1,0:T(8,128)} async-done(((f32[2,1024,256]{2,1,0:T(8,128)}), f32[2,1024,256]{2,1,0:T(8,128)}) %all-reduce.8.cloned.1.call-update) | async-done | bytes 2097168 | tf_op jit(solution)/shard_map/psum | solution.py:36
  291.3 3.3 %broadcast_divide_fusion = f32[2,1024,256]{2,1,0:T(8,128)} fusion(f32[2,1024,256]{2,1,0:T(8,128)} %all-reduce.8.cloned.1.call-done, f32[2,1024]{1,0:T(2,128)S(1)} %get-tuple-element.4), kind=kLoop, calls=%fused_computation.31 | loop fusion | flops 524288 | bytes 4202496 | tf_op jit(solution)/shard_map/div | solution.py:37
  (2 shorter events, 0.0 us)
Async XLA Ops:
  7.2 97.6 %all-reduce.4.cloned.1.call-start = ((), (), s32[]{:S(2)}) async-start(), calls=%async_computation | async-start | bytes 4194304 | tf_op jit(solution)/shard_map/psum | solution.py:36
  11.1 21.4 %copy-start.1 = (f32[2,1024]{1,0:T(2,128)S(1)}, f32[2,1024]{1,0:T(2,128)}, u32[]{:S(2)}) copy-start(f32[2,1024]{1,0:T(2,128)} %param.6) | copy-start | bytes 24580
  11.1 35.4 %copy-start = (bf16[1024,512]{1,0:T(8,128)(2,1)S(1)}, bf16[1024,512]{1,0:T(8,128)(2,1)}, u32[]{:S(2)}) copy-start(bf16[1024,512]{1,0:T(8,128)(2,1)} %param.4) | copy-start | bytes 3145732
  53.4 144.7 %all-reduce.6.cloned.1.call-start = ((), (), s32[]{:S(2)}) async-start(), calls=%async_computation.1 | async-start | bytes 4194304 | tf_op jit(solution)/shard_map/psum | solution.py:36
  147.7 143.6 %all-reduce.8.cloned.1.call-start = ((), (), s32[]{:S(2)}) async-start(), calls=%async_computation.2 | async-start | bytes 4194304 | tf_op jit(solution)/shard_map/psum | solution.py:36
Sparse Core Ops, SparseCore 0:
  53.6 51.1 all-reduce.3
  147.8 50.2 all-reduce.5
  241.0 50.2 all-reduce.7
where the time goes:
time: 302 us; the launch traced here: 301 us
  waiting for transfers between devices  113 us (37%)
  blocking collectives  82.7 us (27%)
  other arithmetic  46.3 us (15%)
  matrix products  43.1 us (14%)
  between operations  13.9 us (5%)
    psum x3, waiting for transfers between devices, local_fit(): counts, stat_sum = lax.psum((counts, stat_sum), 'row')  113 us
    pmax x3, blocking collectives, local_fit(): row_max = lax.pmax(jnp.max(logits, axis=2), 'comp')  37.3 us
    psum x3, blocking collectives, local_fit(): row_sum = lax.psum(jnp.sum(shifted, axis=2), 'comp')  25.7 us
    dot_general x3, matrix products, local_fit(): jnp.einsum('snk,snh->skh', resp_f.astype(jnp.bfloat16), x_fits, preferred...  22.6 us
    dot_general x3, matrix products, local_fit(): jnp.einsum('snh,skh->snk', x_fits, mean_vecs.astype(jnp.bfloat16), prefer...  20.5 us
    psum x3, blocking collectives, local_fit(): counts, stat_sum = lax.psum((counts, stat_sum), 'row')  19.6 us
    reduce_sum x3, other arithmetic, local_fit(): counts = jnp.sum(resp_f, axis=1)  17.7 us
    reduce_sum x3, other arithmetic, local_fit(): row_sum = lax.psum(jnp.sum(shifted, axis=2), 'comp')  17.2 us
  transfers between devices with their start and end apart: 3, of which 3 were waited for; matrix products, arithmetic and copies ran while one was open for 6% of the time, Pallas kernels for 0%

commit v1 on v0

v1 whole, which is shorter than its diff:
```python
import functools

import jax
import jax.numpy as jnp
from jax import lax
from jax.experimental import pallas as pl
from jax.experimental.pallas import tpu as pltpu
from jax.sharding import PartitionSpec as P

EPS_COUNT = 1e-6
PRIOR_ALPHA = 1e-3
LOG2E = 1.4426950408889634
LN2 = 0.6931471805599453
MESH = pl.DeviceIdType.MESH

CORES = 2
TP = 256
NCH = 4


def lse2_parts(parts):
    top = functools.reduce(jnp.maximum, parts)
    total = functools.reduce(jnp.add, [jnp.exp2(p - top) for p in parts])
    return top + jnp.log(total) * LOG2E


def em_kernel(
    comp_size, row_size, sweeps,
    temp_ref, lp_ref, x_hbm, mu_hbm,
    mu_out, lp_out, lse_out,
    xg, mu_own, mub, bcol, e_buf, m_buf, l_buf, s_acc, n_acc, mu_fin, lp_fin, sq_buf,
    pre_buf, bc_src, bc_buf, tot_buf,
    load_sem, y_send, y_recv, z_send, z_recv, sy_send, sy_recv, sz_send, sz_recv, own_send, own_recv,
    pre_send, pre_recv, bc_send, bc_recv, post_send, post_recv,
    fin_send, fin_recv, lpf_send, lpf_recv,
):
    z = lax.axis_index("comp")
    r = lax.axis_index("row")
    y, c = r // CORES, r % CORES
    n_chips = comp_size * row_size // CORES
    y_size = row_size // CORES
    chip = z * y_size + y
    block = x_hbm.shape[0]
    half_dim = x_hbm.shape[1] // 2
    total_pts = block * row_size
    n_own = mub.shape[1]
    total_comp = mu_hbm.shape[1] * comp_size
    tiles = total_pts // TP
    half_tiles = tiles // 2
    half = block // 2
    ch = half // NCH
    sib = {"row": y * CORES + (1 - c)}
    yn = {"row": (1 - y) * CORES + c}
    zpart = z + 1 - 2 * (z % 2)
    zn = {"comp": zpart}

    loads = []
    for s in range(2):
        loads.append(pltpu.make_async_copy(
            x_hbm.at[:, pl.ds(s * half_dim, half_dim)],
            xg.at[s, pl.ds(r * block, block), :], load_sem.at[s]))
        loads.append(pltpu.make_async_copy(
            mu_hbm.at[s, pl.ds(r * n_own, n_own), :], mu_own.at[s], load_sem.at[2 + s]))
    for cp in loads:
        cp.start()

    barrier = pltpu.get_barrier_semaphore()
    pl.semaphore_signal(barrier, inc=1, device_id=sib, device_id_type=MESH)
    for k in range(1, n_chips):
        q = lax.rem(chip + k, n_chips)
        pl.semaphore_signal(
            barrier, inc=1, device_id={"comp": q // y_size, "row": (q % y_size) * CORES + c},
            device_id_type=MESH)
    pl.semaphore_wait(barrier, n_chips)

    def remote(src, dst, send, recv, dev):
        return pltpu.make_async_remote_copy(
            src_ref=src, dst_ref=dst, send_sem=send, recv_sem=recv, device_id=dev, device_id_type=MESH)

    hz = z % 2
    ry = (1 - y) * CORES + c

    def xrows(s, blk, hh, k):
        return xg.at[s, pl.ds(blk * block + hh * half + k * ch, ch), :]

    def y_out(s, k):
        v = xrows(s, r, hz, k)
        return remote(v, v, y_send.at[s, k], y_recv.at[s, k], yn)

    def z_fwd(s, k):
        v = xrows(s, ry, hz, k)
        return remote(v, v, z_send.at[s, k], z_recv.at[s, k], zn)

    def sy_fwd(s, k):
        v = xrows(s, ry, hz, k)
        return remote(v, v, sy_send.at[s, k], sy_recv.at[s, k], sib)

    def sz_fwd(s, k):
        v = xrows(s, ry, 1 - hz, k)
        return remote(v, v, sz_send.at[s, k], sz_recv.at[s, k], sib)

    def own_out(s):
        v = xg.at[s, pl.ds(r * block, block), :]
        return remote(v, v, own_send.at[s], own_recv.at[s], sib)

    for s in range(2):
        loads[2 * s].wait()
        for k in range(NCH):
            y_out(s, k).start()
        own_out(s).start()
    for s in range(2):
        loads[2 * s + 1].wait()

    def col_to_row(col):
        n = col.shape[0]
        eye = lax.broadcasted_iota(jnp.int32, (n, n), 0) == lax.broadcasted_iota(jnp.int32, (n, n), 1)
        return jnp.sum(jnp.where(eye, col, 0.0), axis=0, keepdims=True)

    def row_to_col(row):
        n = row.shape[1]
        eye = lax.broadcasted_iota(jnp.int32, (n, n), 0) == lax.broadcasted_iota(jnp.int32, (n, n), 1)
        return jnp.sum(jnp.where(eye, row, 0.0), axis=1, keepdims=True)

    def set_params(s, mean, logw, t):
        mub[s] = mean.astype(jnp.bfloat16)
        mu_sq = jnp.sum(mean * mean, axis=1, keepdims=True)
        bcol[s] = (logw - temp_ref[t] * mu_sq) * LOG2E

    for s in range(2):
        set_params(s, mu_own[s], row_to_col(lp_ref[s:s + 1, pl.ds(pl.multiple_of(r * n_own, n_own), n_own)]), 0)

    def e_step(s, t):
        scale = temp_ref[t] * (2.0 * LOG2E)
        unroll = 4

        def body(i, _):
            for u in range(unroll):
                tile = i * unroll + u
                x = xg[s, pl.ds(pl.multiple_of(tile * TP, TP), TP), :]
                a = lax.dot_general(mub[s], x, (((1,), (1,)), ((), ())), preferred_element_type=jnp.float32)
                l2 = a * scale + bcol[s]
                m = jnp.max(l2, axis=0, keepdims=True)
                e = jnp.exp2(l2 - m)
                e_buf[s, tile] = e
                rs = jnp.sum(e, axis=0, keepdims=True)
                hh, j = tile // half_tiles, tile % half_tiles
                m_buf[s, hh, pl.ds(j, 1), :] = m
                l_buf[s, hh, pl.ds(j, 1), :] = m + jnp.log(rs) * LOG2E
            return 0

        lax.fori_loop(0, tiles // unroll, body, 0)

    def m_step(s, t):
        idx = 2 * t + s
        unroll = 4
        s_acc[...] = jnp.zeros_like(s_acc)
        n_acc[...] = jnp.zeros_like(n_acc)

        def body(i, _):
            dots, ns = [], []
            for u in range(unroll):
                tile = i * unroll + u
                hh, j = tile // half_tiles, tile % half_tiles
                f = jnp.exp2(m_buf[s, hh, pl.ds(j, 1), :] - tot_buf[idx, hh, pl.ds(j, 1), :])
                resp = e_buf[s, tile] * f
                ns.append(resp[:, :128] + resp[:, 128:])
                x = xg[s, pl.ds(pl.multiple_of(tile * TP, TP), TP), :]
                dots.append(jnp.dot(resp.astype(jnp.bfloat16), x, preferred_element_type=jnp.float32))
            s_acc[...] += functools.reduce(jnp.add, dots)
            n_acc[...] += functools.reduce(jnp.add, ns)
            return 0

        lax.fori_loop(0, tiles // unroll, body, 0)
        cnt = jnp.sum(n_acc[...], axis=1, keepdims=True)
        mean = s_acc[...] / (cnt + EPS_COUNT)
        logw = jnp.log((cnt + PRIOR_ALPHA) / (total_pts + total_comp * PRIOR_ALPHA))
        return mean, logw

    def pre(idx):
        return remote(l_buf.at[idx % 2, 1 - c], pre_buf.at[idx], pre_send.at[idx], pre_recv.at[idx], sib)

    def bcast(idx, k):
        q = lax.rem(chip + k, n_chips)
        return remote(bc_src.at[idx], bc_buf.at[idx, k - 1], bc_send.at[idx, k - 1], bc_recv.at[idx, k - 1],
                      {"comp": q // y_size, "row": (q % y_size) * CORES + c})

    def post(idx):
        v = tot_buf.at[idx, c]
        return remote(v, v, post_send.at[idx], post_recv.at[idx], sib)

    def p2(idx):
        pre(idx).wait()
        bc_src[idx] = lse2_parts([l_buf[idx % 2, c], pre_buf[idx]])
        for k in range(1, n_chips):
            bcast(idx, k).start()

    def p3(idx):
        for k in range(1, n_chips):
            bcast(idx, k).wait()
        tot_buf[idx, c] = lse2_parts([bc_src[idx]] + [bc_buf[idx, k] for k in range(n_chips - 1)])
        post(idx).start()

    for s in range(2):
        own_out(s).wait()
        for k in range(NCH):
            y_out(s, k).wait()
            z_fwd(s, k).start()
            sy_fwd(s, k).start()
        for k in range(NCH):
            z_fwd(s, k).wait()
            sz_fwd(s, k).start()
        for k in range(NCH):
            sy_fwd(s, k).wait()
            sz_fwd(s, k).wait()
        e_step(s, 0)
        pre(s).start()

    ones = jnp.ones((8, half_dim), jnp.bfloat16)
    for s in range(2):
        for j in range(block // TP):
            x = xg[s, pl.ds(pl.multiple_of(r * block + j * TP, TP), TP), :].astype(jnp.float32)
            sq = x * x
            hi = sq.astype(jnp.bfloat16)
            lo = (sq - hi.astype(jnp.float32)).astype(jnp.bfloat16)
            d = functools.partial(lax.dot_general, dimension_numbers=(((1,), (1,)), ((), ())),
                                  preferred_element_type=jnp.float32)
            sq_buf[s, j:j + 1, :] = (d(ones, hi) + d(ones, lo))[0:1]

    def fin(s, d):
        v = mu_fin.at[r, s]
        return remote(v, v, fin_send.at[s, d], fin_recv.at[s, d], sib if d == 0 else yn)

    def fin_fwd(s):
        v = mu_fin.at[ry, s]
        return remote(v, v, fin_send.at[s, 2], fin_recv.at[s, 2], sib)

    def lpf(d):
        v = lp_fin.at[r]
        return remote(v, v, lpf_send.at[d], lpf_recv.at[d], sib if d == 0 else yn)

    def lpf_fwd():
        v = lp_fin.at[ry]
        return remote(v, v, lpf_send.at[2], lpf_recv.at[2], sib)

    p2(0)
    p2(1)
    for t in range(sweeps):
        last = t == sweeps - 1
        for s in range(2):
            idx = 2 * t + s
            p3(idx)
            post(idx).wait()
            mean, logw = m_step(s, t)
            if not last:
                set_params(s, mean, logw, t + 1)
                if s == 1:
                    p2(idx + 1)
                e_step(s, t + 1)
                pre(idx + 2).start()
                if s == 1:
                    p2(idx + 2)
            else:
                mu_fin[r, s] = mean
                lp_fin[r, s:s + 1, :] = col_to_row(logw)
                fin(s, 1).start()
                fin(s, 0).start()
    lpf(1).start()
    lpf(0).start()

    t = sweeps - 1
    blk_tiles = block // TP
    for s in range(2):
        for j in range(blk_tiles):
            tile = r * blk_tiles + j
            row = tot_buf[2 * t + s, tile // half_tiles, pl.ds(tile % half_tiles, 1), :]
            lse_out[s:s + 1, j * TP:(j + 1) * TP] = row * LN2 - temp_ref[t] * sq_buf[s, j:j + 1, :]

    for s in range(2):
        fin(s, 1).wait()
        fin_fwd(s).start()
    lpf(1).wait()
    lpf_fwd().start()
    for s in range(2):
        fin(s, 0).wait()
        fin_fwd(s).wait()
    lpf(0).wait()
    lpf_fwd().wait()
    outs = []
    for q in range(row_size):
        for s in range(2):
            cp = pltpu.make_async_copy(mu_fin.at[q, s], mu_out.at[s, pl.ds(q * n_own, n_own), :],
                                       load_sem.at[4 + 2 * q + s])
            cp.start()
            outs.append(cp)
            lp_out[s:s + 1, q * n_own:(q + 1) * n_own] = lp_fin[q, s:s + 1, :]
    for cp in outs:
        cp.wait()


def solution(mesh):
    comp_size = mesh.shape["comp"]
    row_size = mesh.shape["row"]

    def local_fit(x_local, mu_init, logpi_init, inv_temp):
        block, dim = x_local.shape
        half_dim = dim // 2
        n_local = mu_init.shape[1]
        n_own = n_local // row_size
        total_pts = block * row_size
        tiles = total_pts // TP
        sweeps = inv_temp.shape[0]
        n_chips = comp_size * row_size // CORES
        ni = 2 * sweeps
        ht = tiles // 2
        f32, bf16 = jnp.float32, jnp.bfloat16
        dma = pltpu.SemaphoreType.DMA
        vm = pltpu.VMEM
        scratch = [
            vm((2, total_pts, half_dim), bf16),
            vm((2, n_own, half_dim), f32),
            vm((2, n_own, half_dim), bf16),
            vm((2, n_own, 1), f32),
            vm((2, tiles, n_own, TP), f32),
            vm((2, 2, ht, TP), f32),
            vm((2, 2, ht, TP), f32),
            vm((n_own, half_dim), f32),
            vm((n_own, 128), f32),
            vm((row_size, 2, n_own, half_dim), f32),
            vm((row_size, 2, n_own), f32),
            vm((2, block // TP, TP), f32),
            vm((ni, ht, TP), f32),
            vm((ni, ht, TP), f32),
            vm((ni, n_chips - 1, ht, TP), f32),
            vm((ni, 2, ht, TP), f32),
            dma((4 + 2 * row_size,)),
            dma((2, NCH)), dma((2, NCH)), dma((2, NCH)), dma((2, NCH)),
            dma((2, NCH)), dma((2, NCH)), dma((2, NCH)), dma((2, NCH)),
            dma((2,)), dma((2,)),
            dma((ni,)), dma((ni,)), dma((ni, n_chips - 1)), dma((ni, n_chips - 1)), dma((ni,)), dma((ni,)),
            dma((2, 3)), dma((2, 3)), dma((3,)), dma((3,)),
        ]
        return pl.pallas_call(
            functools.partial(em_kernel, comp_size, row_size, sweeps),
            out_shape=(
                jax.ShapeDtypeStruct((2, n_local, half_dim), f32),
                jax.ShapeDtypeStruct((2, n_local), f32),
                jax.ShapeDtypeStruct((2, block), f32),
            ),
            in_specs=[
                pl.BlockSpec(memory_space=pltpu.SMEM),
                pl.BlockSpec(memory_space=pltpu.VMEM),
                pl.BlockSpec(memory_space=pl.ANY),
                pl.BlockSpec(memory_space=pl.ANY),
            ],
            out_specs=(
                pl.BlockSpec(memory_space=pl.ANY),
                pl.BlockSpec(memory_space=pltpu.VMEM),
                pl.BlockSpec(memory_space=pltpu.VMEM),
            ),
            scratch_shapes=scratch,
            compiler_params=pltpu.CompilerParams(
                collective_id=0, has_side_effects=True, vmem_limit_bytes=56 * 1024 * 1024),
        )(inv_temp, logpi_init, x_local, mu_init)

    return jax.shard_map(
        local_fit,
        mesh=mesh,
        in_specs=(P(("grp", "row"), None), P(None, ("grp", "comp"), None), P(None, ("grp", "comp")), P()),
        out_specs=(P(None, ("grp", "comp"), None), P(None, ("grp", "comp")), P(None, ("grp", "row"))),
        check_vma=False,
    )
```

time: 302 us -> 85.5 us (0.28)
  waiting for transfers between devices: 113 us -> 0 us
  blocking collectives: 82.7 us -> 0 us
  Pallas kernels: 0 us -> 80.4 us
  other arithmetic: 46.3 us -> 0 us
  matrix products: 43.1 us -> 0 us
  between operations: 13.9 us -> 0.66 us
    psum x3 -> x0, waiting for transfers between devices: 113 us -> none  [local_fit(): counts, stat_sum = lax.psum((counts, stat_sum), 'row')]
    pallas_call x0 -> x1, Pallas kernels: none -> 80.4 us  [local_fit(): pl.pallas_call(functools.partial(em_kernel, comp_size, row_size, sweeps),...]
    psum x6 -> x0, blocking collectives: 45.4 us -> none  [the longest x3 25.7 us: local_fit(): row_sum = lax.psum(jnp.sum(shifted, axis=2), 'comp')]
    dot_general x6 -> x0, matrix products: 43.1 us -> none  [the longest x3 22.6 us: local_fit(): jnp.einsum('snk,snh->skh', resp_f.astype(jnp.bfloat16), x_fits, preferred...]
    reduce_sum x9 -> x0, other arithmetic: 41.8 us -> none  [the longest x3 17.7 us: local_fit(): counts = jnp.sum(resp_f, axis=1)]
    pmax x3 -> x0, blocking collectives: 37.3 us -> none  [local_fit(): row_max = lax.pmax(jnp.max(logits, axis=2), 'comp')]
    unnamed x4 -> x7, local copies, waits for them, and re-layouts: 0.01 us -> 4.26 us
    div x1 -> x0, other arithmetic: 3.25 us -> none  [local_fit(): mean_vecs = stat_sum / (counts[:, :, None] + EPS_COUNT)]
  transfers between devices with their start and end apart: 3 -> 0, of which waited for: 3 -> 0; matrix products, arithmetic and copies ran while one was open for 6% -> 0% of each run, Pallas kernels for 0% -> 0%
where the time goes in v1:
time: 85.5 us; the launch traced here: 85.3 us
  Pallas kernels  80.4 us (94%)
  local copies, waits for them, and re-layouts  4.26 us (5%)
    pallas_call x1, Pallas kernels, local_fit(): pl.pallas_call(functools.partial(em_kernel, comp_size, row_size, sweeps),...  80.4 us
    unnamed x7, local copies, waits for them, and re-layouts  4.26 us

profile of v1, /device:TPU:0, one launch (start us, length us, event | category | flops | bytes accessed | tf_op | source)
XLA Modules:
  0.0 85.3 jit_solution(1227004049991360777)
XLA Ops:
  0.6 80.4 %shard_map.67 = (f32[2,1024,256]{2,1,0:T(8,128)}, f32[2,1024]{1,0:T(2,128)}, f32[2,1024]{1,0:T(2,128)}) custom-call(f32[3]{0:T(128)} %temp_ref.1, f32[2,1024]{1,0:T(2,128)} %lp_ref.1, bf16[1024,512]{1,0:T(8,128)(2,1)} %x_hbm.1, f32[2,1024,256]{2,1,0:T(8,128)} %mu_hbm.1), custom_call_target="tpu_custom_call" | custom-call | tf_op jit(solution)/shard_map/pallas_call | solution.py:342
  81.0 0.0 copy-start.1
  81.0 0.0 copy-start
  81.0 3.1 %copy.10 = f32[2,1024,256]{2,1,0:T(8,128)} copy(f32[2,1024,256]{2,1,0:T(8,128)} %get-tuple-element.6) | data formatting | bytes 4194304
  84.1 0.0 copy-done.1
  84.1 0.6 copy.11
  84.7 0.0 copy-done
  84.7 0.6 copy.12
Async XLA Ops:
  81.0 3.1 %copy-start.1 = (f32[2,1024]{1,0:T(2,128)S(1)}, f32[2,1024]{1,0:T(2,128)}, u32[]{:S(2)}) copy-start(f32[2,1024]{1,0:T(2,128)} %get-tuple-element.7) | copy-start | bytes 24580
  81.0 3.7 %copy-start = (f32[2,1024]{1,0:T(2,128)S(1)}, f32[2,1024]{1,0:T(2,128)}, u32[]{:S(2)}) copy-start(f32[2,1024]{1,0:T(2,128)} %get-tuple-element.8) | copy-start | bytes 24580

commit v2 on v0

v2 whole, which is shorter than its diff:
```python
import functools

import jax
import jax.numpy as jnp
from jax import lax
from jax.experimental import pallas as pl
from jax.experimental.pallas import tpu as pltpu
from jax.sharding import PartitionSpec as P

EPS_COUNT = 1e-6
PRIOR_ALPHA = 1e-3
LOG2E = 1.4426950408889634
LN2 = 0.6931471805599453
MESH = pl.DeviceIdType.MESH

CORES = 2
TP = 256
NCK = 16
ND = 8
NR = NCK - ND
DEPTH = 5
LAG = 5
EU = 4


def lse2_parts(parts):
    top = functools.reduce(jnp.maximum, parts)
    total = functools.reduce(jnp.add, [jnp.exp2(p - top) for p in parts])
    return top + jnp.log(total) * LOG2E


def dot_t(a, b):
    return lax.dot_general(a, b, (((1,), (1,)), ((), ())), preferred_element_type=jnp.float32)


def eye_mask(n):
    return lax.broadcasted_iota(jnp.int32, (n, n), 0) == lax.broadcasted_iota(jnp.int32, (n, n), 1)


def col_to_row(col):
    return jnp.sum(jnp.where(eye_mask(col.shape[0]), col, 0.0), axis=0, keepdims=True)


def row_to_col(row):
    return jnp.sum(jnp.where(eye_mask(row.shape[1]), row, 0.0), axis=1, keepdims=True)


def twice(b):
    return jnp.concatenate([b, b], axis=1)


def em_kernel(
    comp_size, row_size, sweeps,
    temp_ref, lp_ref, x_hbm, mu_hbm,
    mu_out, lp_out, lse_out,
    xg, mu_all, mub, bcol, brow, e_buf, m_buf, l_buf, lq_buf, s_acc, n_acc, mu_fin, lp_fin, sq_buf,
    zl_src, zl_buf, pre_buf, bc_src, bc_buf, tot_buf,
    load_sem, y_send, y_recv, z_send, z_recv, sy_send, sy_recv, sz_send, sz_recv, own_send, own_recv,
    zl_send, zl_recv, ag_send, ag_recv,
    pre_send, pre_recv, bc_send, bc_recv, post_send, post_recv,
    mx_send, mx_recv, br_send, br_recv, fin_send, fin_recv, lpf_send, lpf_recv, out_sem,
):
    z = lax.axis_index("comp")
    r = lax.axis_index("row")
    y, c = r // CORES, r % CORES
    n_chips = comp_size * row_size // CORES
    y_size = row_size // CORES
    chip = z * y_size + y
    block = x_hbm.shape[0]
    half_dim = x_hbm.shape[1] // 2
    total_pts = block * row_size
    n_own = mub.shape[2]
    total_comp = mu_hbm.shape[1] * comp_size
    bt = block // TP
    ch = block // NCK
    rs = y * CORES + (1 - c)
    ry = (1 - y) * CORES + c
    sib = {"row": rs}
    yn = {"row": ry}
    yd = {"row": (1 - y) * CORES + (1 - c)}
    zn = {"comp": z + 1 - 2 * (z % 2)}
    hz = z % 2

    def remote(src, dst, send, recv, dev):
        return pltpu.make_async_remote_copy(
            src_ref=src, dst_ref=dst, send_sem=send, recv_sem=recv, device_id=dev, device_id_type=MESH)

    def same(v, send, recv, dev):
        return remote(v, v, send, recv, dev)

    x_loads = [pltpu.make_async_copy(
        x_hbm.at[:, pl.ds(s * half_dim, half_dim)], xg.at[s, pl.ds(r * block, block), :], load_sem.at[s])
        for s in range(2)]
    mu_loads = [pltpu.make_async_copy(mu_hbm.at[s], mu_all.at[s], load_sem.at[2 + s]) for s in range(2)]
    for cp in x_loads + mu_loads:
        cp.start()

    barrier = pltpu.get_barrier_semaphore()
    for dev in (sib, yd):
        pl.semaphore_signal(barrier, inc=1, device_id=dev, device_id_type=MESH)
    for k in range(1, n_chips):
        q = lax.rem(chip + k, n_chips)
        pl.semaphore_signal(
            barrier, inc=1, device_id={"comp": q // y_size, "row": (q % y_size) * CORES + c},
            device_id_type=MESH)
    pl.semaphore_wait(barrier, n_chips + 1)

    def xrows(s, blk, cid):
        return xg.at[s, pl.ds(pl.multiple_of(blk * block + cid * ch, ch), ch), :]

    def cid_y(k):
        return k + hz * (NCK - 1 - 2 * k)

    def cid_z(k):
        return k + (1 - hz) * (NCK - 1 - 2 * k)

    def y_out(j):
        return same(xrows(j // ND, r, cid_y(j % ND)), y_send.at[j], y_recv.at[j], yn)

    def z_fwd(j):
        return same(xrows(j // ND, ry, cid_y(j % ND)), z_send.at[j], z_recv.at[j], zn)

    def sy_fwd(j):
        return same(xrows(j // ND, ry, cid_y(j % ND)), sy_send.at[j], sy_recv.at[j], sib)

    def sz_fwd(j):
        return same(xrows(j // ND, ry, cid_z(j % ND)), sz_send.at[j], sz_recv.at[j], sib)

    def own_out(s):
        return same(xg.at[s, pl.ds(r * block, block), :], own_send.at[s], own_recv.at[s], sib)

    n_steps = 2 * ND + LAG
    comb_end = 8

    def relay(j):
        @pl.when(j < 2 * ND)
        def _():
            y_out(j).wait()

            @pl.when(j + DEPTH < 2 * ND)
            def _():
                y_out(j + DEPTH).start()

            @pl.when(j % ND < NR)
            def _():
                z_fwd(j).start()

            sy_fwd(j).start()

        jz = j - LAG

        @pl.when(jnp.logical_and(jz >= 0, (jz + ND) % ND < NR))
        def _():
            z_fwd(jz).wait()
            sz_fwd(jz).start()

    def relays(a, b):
        def body(j, _):
            relay(j)
            return 0

        lax.fori_loop(a, b, body, 0)

    x_loads[0].wait()
    for j in range(min(DEPTH, ND)):
        y_out(j).start()
    own_out(0).start()
    x_loads[1].wait()
    own_out(1).start()
    for cp in mu_loads:
        cp.wait()

    def set_params(s, slot, mean, logw, t):
        mub[s, slot] = mean.astype(jnp.bfloat16)
        mu_sq = jnp.sum(mean * mean, axis=1, keepdims=True)
        col = (logw - temp_ref[t] * mu_sq) * LOG2E
        bcol[s, slot] = jnp.broadcast_to(col, (n_own, 128))
        return col

    def x_tile(s, tile):
        return xg[s, pl.ds(pl.multiple_of(tile * TP, TP), TP), :]

    def e_tile(s, slot, t, tile):
        a = dot_t(mub[s, slot], x_tile(s, tile))
        l2 = a * (temp_ref[t] * (2.0 * LOG2E)) + twice(bcol[s, slot])
        m = jnp.max(l2, axis=0, keepdims=True)
        e = jnp.exp2(l2 - m)
        return e, m, m + jnp.log(jnp.sum(e, axis=0, keepdims=True)) * LOG2E

    def e_step(s, t, hook=None):
        def body(i, _):
            for u in range(EU):
                tile = i * EU + u
                b, j = i * (EU // bt) + u // bt, u % bt
                e, m, l = e_tile(s, r, t, tile)
                e_buf[s, tile] = e
                m_buf[s, b, j:j + 1, :] = m
                l_buf[s, b, j:j + 1, :] = l
            if hook is not None:
                hook(i)
            return 0

        lax.fori_loop(0, total_pts // (TP * EU), body, 0)

    def acc_zero():
        s_acc[...] = jnp.zeros_like(s_acc)
        n_acc[...] = jnp.zeros_like(n_acc)

    def acc_block(s, b, resp_of):
        dots, ns = [], []
        for u in range(bt):
            resp = resp_of(u)
            ns.append(resp[:, :128] + resp[:, 128:])
            dots.append(jnp.dot(resp.astype(jnp.bfloat16), x_tile(s, b * bt + u), preferred_element_type=jnp.float32))
        s_acc[...] += functools.reduce(jnp.add, dots)
        n_acc[...] += functools.reduce(jnp.add, ns)

    def m_step(s, t):
        idx = 2 * t + s
        acc_zero()

        def body(b, _):
            def resp_of(u):
                f = jnp.exp2(m_buf[s, b, u:u + 1, :] - tot_buf[idx, b, u:u + 1, :])
                return e_buf[s, b * bt + u] * f

            acc_block(s, b, resp_of)
            return 0

        lax.fori_loop(0, row_size, body, 0)

    def mr_block(s, slot, t, b):
        idx = 2 * t + s

        def resp_of(u):
            a = dot_t(mub[s, slot], x_tile(s, b * bt + u))
            return jnp.exp2(a * (temp_ref[t] * (2.0 * LOG2E)) + twice(bcol[s, slot]) - tot_buf[idx, b, u:u + 1, :])

        acc_block(s, b, resp_of)

    def acc_result():
        cnt = jnp.sum(n_acc[...], axis=1, keepdims=True)
        mean = s_acc[...] / (cnt + EPS_COUNT)
        logw = jnp.log((cnt + PRIOR_ALPHA) / (total_pts + total_comp * PRIOR_ALPHA))
        return mean, logw

    def half(ref, k):
        return ref.at[pl.ds(2 * k, 2)]

    def pre(idx):
        return remote(half(l_buf.at[idx % 2], 1 - c), pre_buf.at[idx], pre_send.at[idx], pre_recv.at[idx], sib)

    def bcast(idx, k):
        q = lax.rem(chip + k, n_chips)
        return remote(bc_src.at[idx], bc_buf.at[idx, k - 1], bc_send.at[idx, k - 1], bc_recv.at[idx, k - 1],
                      {"comp": q // y_size, "row": (q % y_size) * CORES + c})

    def post(idx):
        return same(half(tot_buf.at[idx], c), post_send.at[idx], post_recv.at[idx], sib)

    def p2(idx):
        pre(idx).wait()
        bc_src[idx] = lse2_parts([l_buf[idx % 2, pl.ds(2 * c, 2)], pre_buf[idx]])
        for k in range(1, n_chips):
            bcast(idx, k).start()

    def p3(idx):
        for k in range(1, n_chips):
            bcast(idx, k).wait()
        tot_buf[idx, pl.ds(2 * c, 2)] = lse2_parts([bc_src[idx]] + [bc_buf[idx, k] for k in range(n_chips - 1)])
        post(idx).start()

    def zl(s, k):
        return remote(zl_src.at[s], zl_buf.at[s, k - 1], zl_send.at[s, k - 1], zl_recv.at[s, k - 1],
                      {"comp": lax.rem(z + k, comp_size)})

    def ag(s, k):
        return same(tot_buf.at[s, r], ag_send.at[s, k], ag_recv.at[s, k], (sib, yn, yd)[k])

    def orig_fit(s, _):
        def orig_slot(q, _):
            off = pl.multiple_of(q * n_own, n_own)
            set_params(s, q, mu_all[s, pl.ds(off, n_own), :], row_to_col(lp_ref[pl.ds(s, 1), pl.ds(off, n_own)]), 0)
            for u in range(bt):
                _, _, l = e_tile(s, q, 0, r * bt + u)
                lq_buf[q, u:u + 1, :] = l
            return 0

        lax.fori_loop(0, row_size, orig_slot, 0)
        zl_src[s] = lse2_parts([lq_buf[q] for q in range(row_size)])
        for k in range(1, comp_size):
            zl(s, k).start()
        relay(s)
        return 0

    lax.fori_loop(0, 2, orig_fit, 0)

    def comb(s, _):
        relays(2 + (comb_end - 2) // 2 * s, 2 + (comb_end - 2) // 2 * (s + 1))
        for k in range(1, comp_size):
            zl(s, k).wait()
        tot_buf[s, r] = lse2_parts([zl_src[s]] + [zl_buf[s, k] for k in range(comp_size - 1)])
        for k in range(3):
            ag(s, k).start()
        return 0

    lax.fori_loop(0, 2, comb, 0)

    ones = jnp.ones((8, half_dim), jnp.bfloat16)

    def sq_norms(s, _):
        for u in range(bt):
            x = x_tile(s, r * bt + u).astype(jnp.float32)
            sq = x * x
            hi = sq.astype(jnp.bfloat16)
            lo = (sq - hi.astype(jnp.float32)).astype(jnp.bfloat16)
            sq_buf[s, u:u + 1, :] = (dot_t(ones, hi) + dot_t(ones, lo))[0:1]
        return 0

    lax.fori_loop(0, 2, sq_norms, 0)

    def nth_block(k):
        yy = y + (k // 2) * (1 - 2 * y)
        cc = c + (k % 2) * (1 - 2 * c)
        return yy * CORES + cc

    first_end = ND + LAG
    hooks = total_pts // (TP * EU)

    def sweep0(s, _):
        begin = comb_end + s * (first_end + hooks - comb_end)
        relays(begin, begin + 1)
        for k in range(3):
            ag(s, k).wait()
        own_out(s).wait()
        acc_zero()

        def body(k, _):
            @pl.when(k == 2)
            def _():
                relays(begin + 1, first_end + s * (n_steps - first_end))

                def sib_waits(j, _):
                    sy_fwd(j).wait()

                    @pl.when(j % ND < NR)
                    def _():
                        sz_fwd(j).wait()

                    return 0

                lax.fori_loop(s * ND, (s + 1) * ND, sib_waits, 0)

            mr_block(s, r, 0, nth_block(k))
            return 0

        lax.fori_loop(0, row_size, body, 0)
        mean, logw = acc_result()
        set_params(s, r, mean, logw, 1)

        @pl.when(s == 1)
        def _():
            p2(2)

        def hook(i):
            @pl.when(s == 0)
            def _():
                relays(first_end + i, first_end + i + 1)

        e_step(s, 1, hook)
        pre(2 + s).start()

        @pl.when(s == 1)
        def _():
            p2(3)

        return 0

    lax.fori_loop(0, 2, sweep0, 0)

    def mx(s):
        return same(mub.at[s, r], mx_send.at[s], mx_recv.at[s], yn)

    def br(s):
        return same(brow.at[s, r], br_send.at[s], br_recv.at[s], yn)

    def fin(slot, s, k):
        return same(mu_fin.at[slot, s], fin_send.at[s, k], fin_recv.at[s, k], sib)

    def lpf(slot, k):
        return same(lp_fin.at[slot], lpf_send.at[k], lpf_recv.at[k], sib)

    def out(q, s):
        return pltpu.make_async_copy(
            mu_fin.at[q, s], mu_out.at[s, pl.ds(q * n_own, n_own), :], out_sem.at[q, s])

    def sweep(i, _):
        t, s = i // 2, i % 2
        last = t == sweeps - 1
        p3(i)
        post(i).wait()
        m_step(s, t)
        mean, logw = acc_result()

        @pl.when(t < sweeps - 1)
        def _():
            col = set_params(s, r, mean, logw, t + 1)

            @pl.when(t == sweeps - 2)
            def _():
                brow[s, r] = col_to_row(col)

            @pl.when(s == 1)
            def _():
                p2(i + 1)

                @pl.when(t == sweeps - 2)
                def _():
                    mx(0).start()
                    br(0).start()

            e_step(s, t + 1)
            pre(i + 2).start()

            @pl.when(s == 1)
            def _():
                p2(i + 2)

                @pl.when(t == sweeps - 2)
                def _():
                    mx(1).start()
                    br(1).start()

        @pl.when(last)
        def _():
            mu_fin[r, s] = mean
            lp_fin[r, pl.ds(s, 1), :] = col_to_row(logw)
            fin(r, s, 0).start()
            out(r, s).start()
            mx(s).wait()
            br(s).wait()
            bcol[s, ry] = jnp.broadcast_to(row_to_col(brow[s, ry]), (n_own, 128))
            acc_zero()

            def body(b, _):
                mr_block(s, ry, t, b)
                return 0

            lax.fori_loop(0, row_size, body, 0)
            mean2, logw2 = acc_result()
            mu_fin[ry, s] = mean2
            lp_fin[ry, pl.ds(s, 1), :] = col_to_row(logw2)
            fin(ry, s, 1).start()
            out(ry, s).start()

        return 0

    lax.fori_loop(2, 2 * sweeps, sweep, 0)
    lpf(r, 0).start()
    lpf(ry, 1).start()

    t = sweeps - 1
    for s in range(2):
        for j in range(bt):
            lse_out[s:s + 1, j * TP:(j + 1) * TP] = (
                tot_buf[2 * t + s, r, j:j + 1, :] * LN2 - temp_ref[t] * sq_buf[s, j:j + 1, :])

    yds = (1 - y) * CORES + (1 - c)
    for k, slot in ((0, rs), (1, yds)):
        for s in range(2):
            fin((r, ry)[k], s, k).wait()
            out(slot, s).start()
    lpf(r, 0).wait()
    lpf(ry, 1).wait()
    for q in range(row_size):
        lp_out[:, q * n_own:(q + 1) * n_own] = lp_fin[q]
    for q in range(row_size):
        for s in range(2):
            out(q, s).wait()


def solution(mesh):
    comp_size = mesh.shape["comp"]
    row_size = mesh.shape["row"]

    def local_fit(x_local, mu_init, logpi_init, inv_temp):
        block, dim = x_local.shape
        half_dim = dim // 2
        n_local = mu_init.shape[1]
        n_own = n_local // row_size
        total_pts = block * row_size
        tiles = total_pts // TP
        sweeps = inv_temp.shape[0]
        n_chips = comp_size * row_size // CORES
        ni = 2 * sweeps
        bt = block // TP
        f32, bf16 = jnp.float32, jnp.bfloat16
        dma = pltpu.SemaphoreType.DMA
        vm = pltpu.VMEM
        scratch = [
            vm((2, total_pts, half_dim), bf16),
            vm((2, n_local, half_dim), f32),
            vm((2, row_size, n_own, half_dim), bf16),
            vm((2, row_size, n_own, 128), f32),
            vm((2, row_size, 1, n_own), f32),
            vm((2, tiles, n_own, TP), f32),
            vm((2, row_size, bt, TP), f32),
            vm((2, row_size, bt, TP), f32),
            vm((row_size, bt, TP), f32),
            vm((n_own, half_dim), f32),
            vm((n_own, 128), f32),
            vm((row_size, 2, n_own, half_dim), f32),
            vm((row_size, 2, n_own), f32),
            vm((2, bt, TP), f32),
            vm((2, bt, TP), f32),
            vm((2, comp_size - 1, bt, TP), f32),
            vm((ni, 2, bt, TP), f32),
            vm((ni, 2, bt, TP), f32),
            vm((ni, n_chips - 1, 2, bt, TP), f32),
            vm((ni, row_size, bt, TP), f32),
            dma((4,)),
            dma((2 * ND,)), dma((2 * ND,)), dma((2 * ND,)), dma((2 * ND,)),
            dma((2 * ND,)), dma((2 * ND,)), dma((2 * ND,)), dma((2 * ND,)),
            dma((2,)), dma((2,)),
            dma((2, comp_size - 1)), dma((2, comp_size - 1)), dma((2, 3)), dma((2, 3)),
            dma((ni,)), dma((ni,)), dma((ni, n_chips - 1)), dma((ni, n_chips - 1)), dma((ni,)), dma((ni,)),
            dma((2,)), dma((2,)), dma((2,)), dma((2,)),
            dma((2, 2)), dma((2, 2)), dma((2,)), dma((2,)), dma((row_size, 2)),
        ]
        return pl.pallas_call(
            functools.partial(em_kernel, comp_size, row_size, sweeps),
            out_shape=(
                jax.ShapeDtypeStruct((2, n_local, half_dim), f32),
                jax.ShapeDtypeStruct((2, n_local), f32),
                jax.ShapeDtypeStruct((2, block), f32),
            ),
            in_specs=[
                pl.BlockSpec(memory_space=pltpu.SMEM),
                pl.BlockSpec(memory_space=pltpu.VMEM),
                pl.BlockSpec(memory_space=pl.ANY),
                pl.BlockSpec(memory_space=pl.ANY),
            ],
            out_specs=(
                pl.BlockSpec(memory_space=pl.ANY),
                pl.BlockSpec(memory_space=pltpu.VMEM),
                pl.BlockSpec(memory_space=pltpu.VMEM),
            ),
            scratch_shapes=scratch,
            compiler_params=pltpu.CompilerParams(
                collective_id=0, has_side_effects=True, vmem_limit_bytes=56 * 1024 * 1024),
        )(inv_temp, logpi_init, x_local, mu_init)

    return jax.shard_map(
        local_fit,
        mesh=mesh,
        in_specs=(P(("grp", "row"), None), P(None, ("grp", "comp"), None), P(None, ("grp", "comp")), P()),
        out_specs=(P(None, ("grp", "comp"), None), P(None, ("grp", "comp")), P(None, ("grp", "row"))),
        check_vma=False,
    )
```

time: 302 us -> 65.7 us (0.22)
  waiting for transfers between devices: 113 us -> 0 us
  blocking collectives: 82.7 us -> 0 us
  Pallas kernels: 0 us -> 60.5 us
  other arithmetic: 46.3 us -> 0 us
  matrix products: 43.1 us -> 0 us
  between operations: 13.9 us -> 0.66 us
    psum x3 -> x0, waiting for transfers between devices: 113 us -> none  [local_fit(): counts, stat_sum = lax.psum((counts, stat_sum), 'row')]
    pallas_call x0 -> x1, Pallas kernels: none -> 60.5 us  [local_fit(): pl.pallas_call(functools.partial(em_kernel, comp_size, row_size, sweeps),...]
    psum x6 -> x0, blocking collectives: 45.4 us -> none  [the longest x3 25.7 us: local_fit(): row_sum = lax.psum(jnp.sum(shifted, axis=2), 'comp')]
    dot_general x6 -> x0, matrix products: 43.1 us -> none  [the longest x3 22.6 us: local_fit(): jnp.einsum('snk,snh->skh', resp_f.astype(jnp.bfloat16), x_fits, preferred...]
    reduce_sum x9 -> x0, other arithmetic: 41.8 us -> none  [the longest x3 17.7 us: local_fit(): counts = jnp.sum(resp_f, axis=1)]
    pmax x3 -> x0, blocking collectives: 37.3 us -> none  [local_fit(): row_max = lax.pmax(jnp.max(logits, axis=2), 'comp')]
    unnamed x4 -> x7, local copies, waits for them, and re-layouts: 0.01 us -> 4.26 us
    div x1 -> x0, other arithmetic: 3.25 us -> none  [local_fit(): mean_vecs = stat_sum / (counts[:, :, None] + EPS_COUNT)]
  transfers between devices with their start and end apart: 3 -> 0, of which waited for: 3 -> 0; matrix products, arithmetic and copies ran while one was open for 6% -> 0% of each run, Pallas kernels for 0% -> 0%
where the time goes in v2:
time: 65.7 us; the launch traced here: 65.5 us
  Pallas kernels  60.5 us (92%)
  local copies, waits for them, and re-layouts  4.26 us (6%)
  between operations  0.66 us (1%)
    pallas_call x1, Pallas kernels, local_fit(): pl.pallas_call(functools.partial(em_kernel, comp_size, row_size, sweeps),...  60.5 us
    unnamed x7, local copies, waits for them, and re-layouts  4.26 us

profile of v2, /device:TPU:0, one launch (start us, length us, event | category | flops | bytes accessed | tf_op | source)
XLA Modules:
  0.0 65.5 jit_solution(14912001456783100128)
XLA Ops:
  0.6 60.5 %shard_map.67 = (f32[2,1024,256]{2,1,0:T(8,128)}, f32[2,1024]{1,0:T(2,128)}, f32[2,1024]{1,0:T(2,128)}) custom-call(f32[3]{0:T(128)} %temp_ref.1, f32[2,1024]{1,0:T(2,128)} %lp_ref.1, bf16[1024,512]{1,0:T(8,128)(2,1)} %x_hbm.1, f32[2,1024,256]{2,1,0:T(8,128)} %mu_hbm.1), custom_call_target="tpu_custom_call" | custom-call | tf_op jit(solution)/shard_map/pallas_call | solution.py:530
  61.2 0.0 copy-start.1
  61.2 0.0 copy-start
  61.2 3.1 %copy.10 = f32[2,1024,256]{2,1,0:T(8,128)} copy(f32[2,1024,256]{2,1,0:T(8,128)} %get-tuple-element.6) | data formatting | bytes 4194304
  64.3 0.0 copy-done.1
  64.3 0.6 copy.11
  64.9 0.0 copy-done
  64.9 0.6 copy.12
Async XLA Ops:
  61.2 3.1 %copy-start.1 = (f32[2,1024]{1,0:T(2,128)S(1)}, f32[2,1024]{1,0:T(2,128)}, u32[]{:S(2)}) copy-start(f32[2,1024]{1,0:T(2,128)} %get-tuple-element.7) | copy-start | bytes 24580
  61.2 3.7 %copy-start = (f32[2,1024]{1,0:T(2,128)S(1)}, f32[2,1024]{1,0:T(2,128)}, u32[]{:S(2)}) copy-start(f32[2,1024]{1,0:T(2,128)} %get-tuple-element.8) | copy-start | bytes 24580

commit v3 on v2

--- a/solution.py
+++ b/solution.py
@@ -18,9 +18,7 @@
 NCK = 16
 ND = 8
 NR = NCK - ND
-DEPTH = 5
-LAG = 5
-EU = 4
+LAG = 4
 
 
 def lse2_parts(parts):
@@ -55,7 +53,7 @@
     mu_out, lp_out, lse_out,
     xg, mu_all, mub, bcol, brow, e_buf, m_buf, l_buf, lq_buf, s_acc, n_acc, mu_fin, lp_fin, sq_buf,
     zl_src, zl_buf, pre_buf, bc_src, bc_buf, tot_buf,
-    load_sem, y_send, y_recv, z_send, z_recv, sy_send, sy_recv, sz_send, sz_recv, own_send, own_recv,
+    load_sem, near_sem, far_sem, y_send, y_recv, z_send, z_recv, sy_send, sy_recv, sz_send, sz_recv, own_send, own_recv,
     zl_send, zl_recv, ag_send, ag_recv,
     pre_send, pre_recv, bc_send, bc_recv, post_send, post_recv,
     mx_send, mx_recv, br_send, br_recv, fin_send, fin_recv, lpf_send, lpf_recv, out_sem,
@@ -95,15 +93,26 @@
     for cp in x_loads + mu_loads:
         cp.start()
 
+    n_z = (z > 0).astype(jnp.int32) + (z < comp_size - 1).astype(jnp.int32)
+
+    def signal_z(sem):
+        @pl.when(z > 0)
+        def _():
+            pl.semaphore_signal(sem, inc=1, device_id={"comp": z - 1}, device_id_type=MESH)
+
+        @pl.when(z < comp_size - 1)
+        def _():
+            pl.semaphore_signal(sem, inc=1, device_id={"comp": z + 1}, device_id_type=MESH)
+
+    def signal_near(sem):
+        for dev in (sib, yn):
+            pl.semaphore_signal(sem, inc=1, device_id=dev, device_id_type=MESH)
+        signal_z(sem)
+
     barrier = pltpu.get_barrier_semaphore()
-    for dev in (sib, yd):
-        pl.semaphore_signal(barrier, inc=1, device_id=dev, device_id_type=MESH)
-    for k in range(1, n_chips):
-        q = lax.rem(chip + k, n_chips)
-        pl.semaphore_signal(
-            barrier, inc=1, device_id={"comp": q // y_size, "row": (q % y_size) * CORES + c},
-            device_id_type=MESH)
-    pl.semaphore_wait(barrier, n_chips + 1)
+    signal_near(barrier)
+    pl.semaphore_wait(barrier, 2 + n_z)
+    signal_near(near_sem)
 
     def xrows(s, blk, cid):
         return xg.at[s, pl.ds(pl.multiple_of(blk * block + cid * ch, ch), ch), :]
@@ -131,15 +140,12 @@
 
     n_steps = 2 * ND + LAG
     comb_end = 8
+    first_end = ND + LAG
 
     def relay(j):
         @pl.when(j < 2 * ND)
         def _():
             y_out(j).wait()
-
-            @pl.when(j + DEPTH < 2 * ND)
-            def _():
-                y_out(j + DEPTH).start()
 
             @pl.when(j % ND < NR)
             def _():
@@ -162,7 +168,7 @@
         lax.fori_loop(a, b, body, 0)
 
     x_loads[0].wait()
-    for j in range(min(DEPTH, ND)):
+    for j in range(ND):
         y_out(j).start()
     own_out(0).start()
     x_loads[1].wait()
@@ -187,20 +193,31 @@
         e = jnp.exp2(l2 - m)
         return e, m, m + jnp.log(jnp.sum(e, axis=0, keepdims=True)) * LOG2E
 
-    def e_step(s, t, hook=None):
+    def sib_half_first(i):
+        return 2 * ((1 - c) + (i // 2) * (2 * c - 1)) + i % 2
+
+    def own_half_first(i):
+        return 2 * (c + (i // 2) * (1 - 2 * c)) + i % 2
+
+    def e_step(s, t, idx, hook=None):
         def body(i, _):
-            for u in range(EU):
-                tile = i * EU + u
-                b, j = i * (EU // bt) + u // bt, u % bt
-                e, m, l = e_tile(s, r, t, tile)
-                e_buf[s, tile] = e
-                m_buf[s, b, j:j + 1, :] = m
-                l_buf[s, b, j:j + 1, :] = l
+            b = sib_half_first(i)
+            for u in range(bt):
+                e, m, l = e_tile(s, r, t, b * bt + u)
+                e_buf[s, b * bt + u] = e
+                m_buf[s, b, u:u + 1, :] = m
+                l_buf[s, b, u:u + 1, :] = l
+
+            @pl.when(i == 1)
+            def _():
+                pre(idx).start()
+
             if hook is not None:
                 hook(i)
             return 0
 
-        lax.fori_loop(0, total_pts // (TP * EU), body, 0)
+        lax.fori_loop(0, row_size, body, 0)
+        p2(idx)
 
     def acc_zero():
         s_acc[...] = jnp.zeros_like(s_acc)
@@ -219,7 +236,13 @@
         idx = 2 * t + s
         acc_zero()
 
-        def body(b, _):
+        def body(i, _):
+            @pl.when(i == 2)
+            def _():
+                post(idx).wait()
+
+            b = own_half_first(i)
+
             def resp_of(u):
                 f = jnp.exp2(m_buf[s, b, u:u + 1, :] - tot_buf[idx, b, u:u + 1, :])
                 return e_buf[s, b * bt + u] * f
@@ -284,10 +307,21 @@
             for u in range(bt):
                 _, _, l = e_tile(s, q, 0, r * bt + u)
                 lq_buf[q, u:u + 1, :] = l
+
+            @pl.when(jnp.logical_and(s == 0, q == 1))
+            def _():
+                pl.semaphore_wait(near_sem, 2 + n_z)
+                signal_z(far_sem)
+
             return 0
 
         lax.fori_loop(0, row_size, orig_slot, 0)
         zl_src[s] = lse2_parts([lq_buf[q] for q in range(row_size)])
+
+        @pl.when(s == 0)
+        def _():
+            pl.semaphore_wait(far_sem, n_z)
+
         for k in range(1, comp_size):
             zl(s, k).start()
         relay(s)
@@ -302,9 +336,74 @@
         tot_buf[s, r] = lse2_parts([zl_src[s]] + [zl_buf[s, k] for k in range(comp_size - 1)])
         for k in range(3):
             ag(s, k).start()
+
+        @pl.when(s == 0)
+        def _():
+            def send(j, _):
+                y_out(j).start()
+                return 0
+
+            lax.fori_loop(ND, 2 * ND, send, 0)
+
         return 0
 
     lax.fori_loop(0, 2, comb, 0)
+
+    def nth_block(k):
+        yy = y + (k // 2) * (1 - 2 * y)
+        cc = c + (k % 2) * (1 - 2 * c)
+        return yy * CORES + cc
+
+    def sweep0(s, _):
+        @pl.when(s == 0)
+        def _():
+            relays(comb_end, first_end)
+
+        for k in range(3):
+            ag(s, k).wait()
+        own_out(s).wait()
+        acc_zero()
+
+        def sib_waits(j, _):
+            sy_fwd(j).wait()
+
+            @pl.when(j % ND < NR)
+            def _():
+                sz_fwd(j).wait()
+
+            return 0
+
+        @pl.when(s == 0)
+        def _():
+            lax.fori_loop(0, ND, sib_waits, 0)
+
+        def body(k, _):
+            @pl.when(jnp.logical_and(s == 1, k == 2))
+            def _():
+                relays(first_end + 6, n_steps)
+                lax.fori_loop(ND, 2 * ND, sib_waits, 0)
+
+            mr_block(s, r, 0, nth_block(k))
+
+            @pl.when(s == 0)
+            def _():
+                relay(first_end + k)
+
+            return 0
+
+        lax.fori_loop(0, row_size, body, 0)
+        mean, logw = acc_result()
+        set_params(s, r, mean, logw, 1)
+
+        def hook(i):
+            @pl.when(jnp.logical_and(s == 0, i < 2))
+            def _():
+                relay(first_end + 4 + i)
+
+        e_step(s, 1, 2 + s, hook)
+        return 0
+
+    lax.fori_loop(0, 2, sweep0, 0)
 
     ones = jnp.ones((8, half_dim), jnp.bfloat16)
 
@@ -319,65 +418,6 @@
 
     lax.fori_loop(0, 2, sq_norms, 0)
 
-    def nth_block(k):
-        yy = y + (k // 2) * (1 - 2 * y)
-        cc = c + (k % 2) * (1 - 2 * c)
-        return yy * CORES + cc
-
-    first_end = ND + LAG
-    hooks = total_pts // (TP * EU)
-
-    def sweep0(s, _):
-        begin = comb_end + s * (first_end + hooks - comb_end)
-        relays(begin, begin + 1)
-        for k in range(3):
-            ag(s, k).wait()
-        own_out(s).wait()
-        acc_zero()
-
-        def body(k, _):
-            @pl.when(k == 2)
-            def _():
-                relays(begin + 1, first_end + s * (n_steps - first_end))
-
-                def sib_waits(j, _):
-                    sy_fwd(j).wait()
-
-                    @pl.when(j % ND < NR)
-                    def _():
-                        sz_fwd(j).wait()
-
-                    return 0
-
-                lax.fori_loop(s * ND, (s + 1) * ND, sib_waits, 0)
-
-            mr_block(s, r, 0, nth_block(k))
-            return 0
-
-        lax.fori_loop(0, row_size, body, 0)
-        mean, logw = acc_result()
-        set_params(s, r, mean, logw, 1)
-
-        @pl.when(s == 1)
-        def _():
-            p2(2)
-
-        def hook(i):
-            @pl.when(s == 0)
-            def _():
-                relays(first_end + i, first_end + i + 1)
-
-        e_step(s, 1, hook)
-        pre(2 + s).start()
-
-        @pl.when(s == 1)
-        def _():
-            p2(3)
-
-        return 0
-
-    lax.fori_loop(0, 2, sweep0, 0)
-
     def mx(s):
         return same(mub.at[s, r], mx_send.at[s], mx_recv.at[s], yn)
 
@@ -398,7 +438,6 @@
         t, s = i // 2, i % 2
         last = t == sweeps - 1
         p3(i)
-        post(i).wait()
         m_step(s, t)
         mean, logw = acc_result()
 
@@ -410,26 +449,12 @@
             def _():
                 brow[s, r] = col_to_row(col)
 
-            @pl.when(s == 1)
-            def _():
-                p2(i + 1)
-
-                @pl.when(t == sweeps - 2)
-                def _():
-                    mx(0).start()
-                    br(0).start()
-
-            e_step(s, t + 1)
-            pre(i + 2).start()
-
-            @pl.when(s == 1)
-            def _():
-                p2(i + 2)
-
-                @pl.when(t == sweeps - 2)
-                def _():
-                    mx(1).start()
-                    br(1).start()
+            e_step(s, t + 1, i + 2)
+
+            @pl.when(t == sweeps - 2)
+            def _():
+                mx(s).start()
+                br(s).start()
 
         @pl.when(last)
         def _():
@@ -518,7 +543,7 @@
             vm((ni, 2, bt, TP), f32),
             vm((ni, n_chips - 1, 2, bt, TP), f32),
             vm((ni, row_size, bt, TP), f32),
-            dma((4,)),
+            dma((4,)), pltpu.SemaphoreType.REGULAR, pltpu.SemaphoreType.REGULAR,
             dma((2 * ND,)), dma((2 * ND,)), dma((2 * ND,)), dma((2 * ND,)),
             dma((2 * ND,)), dma((2 * ND,)), dma((2 * ND,)), dma((2 * ND,)),
             dma((2,)), dma((2,)),

time: 65.7 us -> 59.7 us (0.909)
  Pallas kernels: 60.5 us -> 54.6 us
    pallas_call x1, Pallas kernels: 60.5 us -> 54.6 us  [local_fit(): pl.pallas_call(functools.partial(em_kernel, comp_size, row_size, sweeps),...]
where the time goes in v3:
time: 59.7 us; the launch traced here: 59.5 us
  Pallas kernels  54.6 us (91%)
  local copies, waits for them, and re-layouts  4.26 us (7%)
  between operations  0.66 us (1%)
    pallas_call x1, Pallas kernels, local_fit(): pl.pallas_call(functools.partial(em_kernel, comp_size, row_size, sweeps),...  54.6 us
    unnamed x7, local copies, waits for them, and re-layouts  4.26 us

profile of v3, /device:TPU:0, one launch (start us, length us, event | category | flops | bytes accessed | tf_op | source)
XLA Modules:
  0.0 59.5 jit_solution(5525194162670142105)
XLA Ops:
  0.6 54.6 %shard_map.67 = (f32[2,1024,256]{2,1,0:T(8,128)}, f32[2,1024]{1,0:T(2,128)}, f32[2,1024]{1,0:T(2,128)}) custom-call(f32[3]{0:T(128)} %temp_ref.1, f32[2,1024]{1,0:T(2,128)} %lp_ref.1, bf16[1024,512]{1,0:T(8,128)(2,1)} %x_hbm.1, f32[2,1024,256]{2,1,0:T(8,128)} %mu_hbm.1), custom_call_target="tpu_custom_call" | custom-call | tf_op jit(solution)/shard_map/pallas_call | solution.py:555
  55.2 0.0 copy-start.1
  55.2 0.0 copy-start
  55.2 3.1 %copy.10 = f32[2,1024,256]{2,1,0:T(8,128)} copy(f32[2,1024,256]{2,1,0:T(8,128)} %get-tuple-element.6) | data formatting | bytes 4194304
  58.3 0.0 copy-done.1
  58.3 0.6 %copy.11 = f32[2,1024]{1,0:T(2,128)} copy(f32[2,1024]{1,0:T(2,128)S(1)} %copy-done.1) | data formatting | bytes 16384
  58.9 0.0 copy-done
  58.9 0.6 %copy.12 = f32[2,1024]{1,0:T(2,128)} copy(f32[2,1024]{1,0:T(2,128)S(1)} %copy-done) | data formatting | bytes 16384
Async XLA Ops:
  55.2 3.1 %copy-start.1 = (f32[2,1024]{1,0:T(2,128)S(1)}, f32[2,1024]{1,0:T(2,128)}, u32[]{:S(2)}) copy-start(f32[2,1024]{1,0:T(2,128)} %get-tuple-element.7) | copy-start | bytes 24580
  55.2 3.7 %copy-start = (f32[2,1024]{1,0:T(2,128)S(1)}, f32[2,1024]{1,0:T(2,128)}, u32[]{:S(2)}) copy-start(f32[2,1024]{1,0:T(2,128)} %get-tuple-element.8) | copy-start | bytes 24580

commit v4 on v3

--- a/solution.py
+++ b/solution.py
@@ -51,12 +51,12 @@
     comp_size, row_size, sweeps,
     temp_ref, lp_ref, x_hbm, mu_hbm,
     mu_out, lp_out, lse_out,
-    xg, mu_all, mub, bcol, brow, e_buf, m_buf, l_buf, lq_buf, s_acc, n_acc, mu_fin, lp_fin, sq_buf,
+    xg, mu_all, mub, bcol, brow, e_buf, m_buf, l_buf, lq_buf, s_acc, n_acc, lp_fin, sq_buf,
     zl_src, zl_buf, pre_buf, bc_src, bc_buf, tot_buf,
     load_sem, near_sem, far_sem, y_send, y_recv, z_send, z_recv, sy_send, sy_recv, sz_send, sz_recv, own_send, own_recv,
     zl_send, zl_recv, ag_send, ag_recv,
     pre_send, pre_recv, bc_send, bc_recv, post_send, post_recv,
-    mx_send, mx_recv, br_send, br_recv, fin_send, fin_recv, lpf_send, lpf_recv, out_sem,
+    mx_send, mx_recv, br_send, br_recv, fin_send, fin_recv, lpf_send, lpf_recv,
 ):
     z = lax.axis_index("comp")
     r = lax.axis_index("row")
@@ -139,7 +139,7 @@
         return same(xg.at[s, pl.ds(r * block, block), :], own_send.at[s], own_recv.at[s], sib)
 
     n_steps = 2 * ND + LAG
-    comb_end = 8
+    comb_end = 10
     first_end = ND + LAG
 
     def relay(j):
@@ -193,22 +193,19 @@
         e = jnp.exp2(l2 - m)
         return e, m, m + jnp.log(jnp.sum(e, axis=0, keepdims=True)) * LOG2E
 
-    def sib_half_first(i):
-        return 2 * ((1 - c) + (i // 2) * (2 * c - 1)) + i % 2
-
-    def own_half_first(i):
-        return 2 * (c + (i // 2) * (1 - 2 * c)) + i % 2
+    def tiles_of(half_id):
+        return [(2 * half_id + k // bt, k % bt) for k in range(2 * bt)]
 
     def e_step(s, t, idx, hook=None):
         def body(i, _):
-            b = sib_half_first(i)
-            for u in range(bt):
+            h = (1 - c) + i * (2 * c - 1)
+            for b, u in tiles_of(h):
                 e, m, l = e_tile(s, r, t, b * bt + u)
                 e_buf[s, b * bt + u] = e
                 m_buf[s, b, u:u + 1, :] = m
                 l_buf[s, b, u:u + 1, :] = l
 
-            @pl.when(i == 1)
+            @pl.when(i == 0)
             def _():
                 pre(idx).start()
 
@@ -216,17 +213,17 @@
                 hook(i)
             return 0
 
-        lax.fori_loop(0, row_size, body, 0)
+        lax.fori_loop(0, 2, body, 0)
         p2(idx)
 
     def acc_zero():
         s_acc[...] = jnp.zeros_like(s_acc)
         n_acc[...] = jnp.zeros_like(n_acc)
 
-    def acc_block(s, b, resp_of):
+    def acc_tiles(s, tiles, resp_of):
         dots, ns = [], []
-        for u in range(bt):
-            resp = resp_of(u)
+        for b, u in tiles:
+            resp = resp_of(b, u)
             ns.append(resp[:, :128] + resp[:, 128:])
             dots.append(jnp.dot(resp.astype(jnp.bfloat16), x_tile(s, b * bt + u), preferred_element_type=jnp.float32))
         s_acc[...] += functools.reduce(jnp.add, dots)
@@ -237,29 +234,27 @@
         acc_zero()
 
         def body(i, _):
-            @pl.when(i == 2)
+            @pl.when(i == 1)
             def _():
                 post(idx).wait()
 
-            b = own_half_first(i)
-
-            def resp_of(u):
+            def resp_of(b, u):
                 f = jnp.exp2(m_buf[s, b, u:u + 1, :] - tot_buf[idx, b, u:u + 1, :])
                 return e_buf[s, b * bt + u] * f
 
-            acc_block(s, b, resp_of)
-            return 0
-
-        lax.fori_loop(0, row_size, body, 0)
-
-    def mr_block(s, slot, t, b):
+            acc_tiles(s, tiles_of(c + i * (1 - 2 * c)), resp_of)
+            return 0
+
+        lax.fori_loop(0, 2, body, 0)
+
+    def mr_half(s, slot, t, half_id):
         idx = 2 * t + s
 
-        def resp_of(u):
+        def resp_of(b, u):
             a = dot_t(mub[s, slot], x_tile(s, b * bt + u))
             return jnp.exp2(a * (temp_ref[t] * (2.0 * LOG2E)) + twice(bcol[s, slot]) - tot_buf[idx, b, u:u + 1, :])
 
-        acc_block(s, b, resp_of)
+        acc_tiles(s, tiles_of(half_id), resp_of)
 
     def acc_result():
         cnt = jnp.sum(n_acc[...], axis=1, keepdims=True)
@@ -301,21 +296,27 @@
         return same(tot_buf.at[s, r], ag_send.at[s, k], ag_recv.at[s, k], (sib, yn, yd)[k])
 
     def orig_fit(s, _):
-        def orig_slot(q, _):
-            off = pl.multiple_of(q * n_own, n_own)
-            set_params(s, q, mu_all[s, pl.ds(off, n_own), :], row_to_col(lp_ref[pl.ds(s, 1), pl.ds(off, n_own)]), 0)
-            for u in range(bt):
-                _, _, l = e_tile(s, q, 0, r * bt + u)
-                lq_buf[q, u:u + 1, :] = l
-
-            @pl.when(jnp.logical_and(s == 0, q == 1))
+        def orig_slots(p, _):
+            for k in range(2):
+                q = 2 * p + k
+                off = pl.multiple_of(q * n_own, n_own)
+                set_params(s, q, mu_all[s, pl.ds(off, n_own), :], row_to_col(lp_ref[pl.ds(s, 1), pl.ds(off, n_own)]), 0)
+                for u in range(bt):
+                    _, _, l = e_tile(s, q, 0, r * bt + u)
+                    lq_buf[q, u:u + 1, :] = l
+
+            @pl.when(jnp.logical_and(s == 0, p == 0))
             def _():
                 pl.semaphore_wait(near_sem, 2 + n_z)
                 signal_z(far_sem)
 
-            return 0
-
-        lax.fori_loop(0, row_size, orig_slot, 0)
+            @pl.when(s == 1)
+            def _():
+                relays(2 * p, 2 * p + 2)
+
+            return 0
+
+        lax.fori_loop(0, row_size // 2, orig_slots, 0)
         zl_src[s] = lse2_parts([lq_buf[q] for q in range(row_size)])
 
         @pl.when(s == 0)
@@ -324,13 +325,22 @@
 
         for k in range(1, comp_size):
             zl(s, k).start()
-        relay(s)
         return 0
 
     lax.fori_loop(0, 2, orig_fit, 0)
 
+    def y_sends(a, b):
+        def send(j, _):
+            y_out(j).start()
+            return 0
+
+        lax.fori_loop(a, b, send, 0)
+
+    early = ND + 3
+    y_sends(ND, early)
+
     def comb(s, _):
-        relays(2 + (comb_end - 2) // 2 * s, 2 + (comb_end - 2) // 2 * (s + 1))
+        relays(4 + 3 * s, 7 + 3 * s)
         for k in range(1, comp_size):
             zl(s, k).wait()
         tot_buf[s, r] = lse2_parts([zl_src[s]] + [zl_buf[s, k] for k in range(comp_size - 1)])
@@ -339,20 +349,11 @@
 
         @pl.when(s == 0)
         def _():
-            def send(j, _):
-                y_out(j).start()
-                return 0
-
-            lax.fori_loop(ND, 2 * ND, send, 0)
+            y_sends(early, 2 * ND)
 
         return 0
 
     lax.fori_loop(0, 2, comb, 0)
-
-    def nth_block(k):
-        yy = y + (k // 2) * (1 - 2 * y)
-        cc = c + (k % 2) * (1 - 2 * c)
-        return yy * CORES + cc
 
     def sweep0(s, _):
         @pl.when(s == 0)
@@ -378,27 +379,27 @@
             lax.fori_loop(0, ND, sib_waits, 0)
 
         def body(k, _):
-            @pl.when(jnp.logical_and(s == 1, k == 2))
+            @pl.when(jnp.logical_and(s == 1, k == 1))
             def _():
                 relays(first_end + 6, n_steps)
                 lax.fori_loop(ND, 2 * ND, sib_waits, 0)
 
-            mr_block(s, r, 0, nth_block(k))
+            mr_half(s, r, 0, y + k * (1 - 2 * y))
 
             @pl.when(s == 0)
             def _():
-                relay(first_end + k)
-
-            return 0
-
-        lax.fori_loop(0, row_size, body, 0)
+                relays(first_end + 2 * k, first_end + 2 * k + 2)
+
+            return 0
+
+        lax.fori_loop(0, 2, body, 0)
         mean, logw = acc_result()
         set_params(s, r, mean, logw, 1)
 
         def hook(i):
-            @pl.when(jnp.logical_and(s == 0, i < 2))
-            def _():
-                relay(first_end + 4 + i)
+            @pl.when(jnp.logical_and(s == 0, i == 0))
+            def _():
+                relays(first_end + 4, first_end + 6)
 
         e_step(s, 1, 2 + s, hook)
         return 0
@@ -424,15 +425,14 @@
     def br(s):
         return same(brow.at[s, r], br_send.at[s], br_recv.at[s], yn)
 
+    def mean_rows(slot, s):
+        return mu_out.at[s, pl.ds(pl.multiple_of(slot * n_own, n_own), n_own), :]
+
     def fin(slot, s, k):
-        return same(mu_fin.at[slot, s], fin_send.at[s, k], fin_recv.at[s, k], sib)
+        return same(mean_rows(slot, s), fin_send.at[s, k], fin_recv.at[s, k], sib)
 
     def lpf(slot, k):
         return same(lp_fin.at[slot], lpf_send.at[k], lpf_recv.at[k], sib)
-
-    def out(q, s):
-        return pltpu.make_async_copy(
-            mu_fin.at[q, s], mu_out.at[s, pl.ds(q * n_own, n_own), :], out_sem.at[q, s])
 
     def sweep(i, _):
         t, s = i // 2, i % 2
@@ -458,25 +458,23 @@
 
         @pl.when(last)
         def _():
-            mu_fin[r, s] = mean
+            mean_rows(r, s)[...] = mean
             lp_fin[r, pl.ds(s, 1), :] = col_to_row(logw)
             fin(r, s, 0).start()
-            out(r, s).start()
             mx(s).wait()
             br(s).wait()
             bcol[s, ry] = jnp.broadcast_to(row_to_col(brow[s, ry]), (n_own, 128))
             acc_zero()
 
-            def body(b, _):
-                mr_block(s, ry, t, b)
+            def body(h, _):
+                mr_half(s, ry, t, h)
                 return 0
 
-            lax.fori_loop(0, row_size, body, 0)
+            lax.fori_loop(0, 2, body, 0)
             mean2, logw2 = acc_result()
-            mu_fin[ry, s] = mean2
+            mean_rows(ry, s)[...] = mean2
             lp_fin[ry, pl.ds(s, 1), :] = col_to_row(logw2)
             fin(ry, s, 1).start()
-            out(ry, s).start()
 
         return 0
 
@@ -490,18 +488,13 @@
             lse_out[s:s + 1, j * TP:(j + 1) * TP] = (
                 tot_buf[2 * t + s, r, j:j + 1, :] * LN2 - temp_ref[t] * sq_buf[s, j:j + 1, :])
 
-    yds = (1 - y) * CORES + (1 - c)
-    for k, slot in ((0, rs), (1, yds)):
+    for k in range(2):
         for s in range(2):
             fin((r, ry)[k], s, k).wait()
-            out(slot, s).start()
     lpf(r, 0).wait()
     lpf(ry, 1).wait()
     for q in range(row_size):
         lp_out[:, q * n_own:(q + 1) * n_own] = lp_fin[q]
-    for q in range(row_size):
-        for s in range(2):
-            out(q, s).wait()
 
 
 def solution(mesh):
@@ -534,7 +527,6 @@
             vm((row_size, bt, TP), f32),
             vm((n_own, half_dim), f32),
             vm((n_own, 128), f32),
-            vm((row_size, 2, n_own, half_dim), f32),
             vm((row_size, 2, n_own), f32),
             vm((2, bt, TP), f32),
             vm((2, bt, TP), f32),
@@ -550,26 +542,18 @@
             dma((2, comp_size - 1)), dma((2, comp_size - 1)), dma((2, 3)), dma((2, 3)),
             dma((ni,)), dma((ni,)), dma((ni, n_chips - 1)), dma((ni, n_chips - 1)), dma((ni,)), dma((ni,)),
             dma((2,)), dma((2,)), dma((2,)), dma((2,)),
-            dma((2, 2)), dma((2, 2)), dma((2,)), dma((2,)), dma((row_size, 2)),
+            dma((2, 2)), dma((2, 2)), dma((2,)), dma((2,)),
         ]
         return pl.pallas_call(
             functools.partial(em_kernel, comp_size, row_size, sweeps),
-            out_shape=(
-                jax.ShapeDtypeStruct((2, n_local, half_dim), f32),
-                jax.ShapeDtypeStruct((2, n_local), f32),
-                jax.ShapeDtypeStruct((2, block), f32),
-            ),
+            out_shape=(vm((2, n_local, half_dim), f32), vm((2, n_local), f32), vm((2, block), f32)),
             in_specs=[
                 pl.BlockSpec(memory_space=pltpu.SMEM),
                 pl.BlockSpec(memory_space=pltpu.VMEM),
                 pl.BlockSpec(memory_space=pl.ANY),
                 pl.BlockSpec(memory_space=pl.ANY),
             ],
-            out_specs=(
-                pl.BlockSpec(memory_space=pl.ANY),
-                pl.BlockSpec(memory_space=pltpu.VMEM),
-                pl.BlockSpec(memory_space=pltpu.VMEM),
-            ),
+            out_specs=(pl.BlockSpec(memory_space=pltpu.VMEM),) * 3,
             scratch_shapes=scratch,
             compiler_params=pltpu.CompilerParams(
                 collective_id=0, has_side_effects=True, vmem_limit_bytes=56 * 1024 * 1024),

time: 59.7 us -> 52.1 us (0.87)
  Pallas kernels: 54.6 us -> 48.7 us
  local copies, waits for them, and re-layouts: 4.26 us -> 2.52 us
    pallas_call x1, Pallas kernels: 54.6 us -> 48.7 us  [local_fit(): pl.pallas_call(functools.partial(em_kernel, comp_size, row_size, sweeps),...]
    unnamed x7 -> x3, local copies, waits for them, and re-layouts: 4.26 us -> 2.52 us
where the time goes in v4:
time: 52.1 us; the launch traced here: 51.9 us
  Pallas kernels  48.7 us (93%)
  local copies, waits for them, and re-layouts  2.52 us (5%)
  between operations  0.64 us (1%)
    pallas_call x1, Pallas kernels, local_fit(): pl.pallas_call(functools.partial(em_kernel, comp_size, row_size, sweeps),...  48.7 us
    unnamed x3, local copies, waits for them, and re-layouts  2.52 us

profile of v4, /device:TPU:0, one launch (start us, length us, event | category | flops | bytes accessed | tf_op | source)
XLA Modules:
  0.0 51.9 jit_solution(4031097624489005975)
XLA Ops:
  0.6 48.7 %shard_map.67 = (f32[2,1024,256]{2,1,0:T(8,128)S(1)}, f32[2,1024]{1,0:T(2,128)S(1)}, f32[2,1024]{1,0:T(2,128)S(1)}) custom-call(f32[3]{0:T(128)} %temp_ref.1, f32[2,1024]{1,0:T(2,128)} %lp_ref.1, bf16[1024,512]{1,0:T(8,128)(2,1)} %x_hbm.1, f32[2,1024,256]{2,1,0:T(8,128)} %mu_hbm.1), custom_call_target="tpu_custom_call" | custom-call | tf_op jit(solution)/shard_map/pallas_call | solution.py:547
  49.4 1.3 %copy.10 = f32[2,1024,256]{2,1,0:T(8,128)} copy(f32[2,1024,256]{2,1,0:T(8,128)S(1)} %get-tuple-element.3) | data formatting | bytes 4194304
  50.7 0.6 %copy.11 = f32[2,1024]{1,0:T(2,128)} copy(f32[2,1024]{1,0:T(2,128)S(1)} %get-tuple-element.4) | data formatting | bytes 16384
  51.3 0.6 %copy.12 = f32[2,1024]{1,0:T(2,128)} copy(f32[2,1024]{1,0:T(2,128)S(1)} %get-tuple-element.5) | data formatting | bytes 16384

commit v5 on v4

--- a/solution.py
+++ b/solution.py
@@ -17,8 +17,6 @@
 TP = 256
 NCK = 16
 ND = 8
-NR = NCK - ND
-LAG = 4
 
 
 def lse2_parts(parts):
@@ -45,6 +43,14 @@
 
 def twice(b):
     return jnp.concatenate([b, b], axis=1)
+
+
+def write_kernel(a, b, c, a_out, b_out, c_out, sems):
+    copies = [pltpu.make_async_copy(v, o, sems.at[k]) for k, (v, o) in enumerate(((a, a_out), (b, b_out), (c, c_out)))]
+    for cp in copies:
+        cp.start()
+    for cp in copies:
+        cp.wait()
 
 
 def em_kernel(
@@ -124,48 +130,48 @@
         return k + (1 - hz) * (NCK - 1 - 2 * k)
 
     def y_out(j):
-        return same(xrows(j // ND, r, cid_y(j % ND)), y_send.at[j], y_recv.at[j], yn)
+        return same(xrows(j // ND, r, cid_y(j % ND)), y_send.at[j // ND], y_recv.at[j], yn)
 
     def z_fwd(j):
-        return same(xrows(j // ND, ry, cid_y(j % ND)), z_send.at[j], z_recv.at[j], zn)
+        return same(xrows(j // ND, ry, cid_y(j % ND)), z_send.at[j // ND], z_recv.at[j], zn)
 
     def sy_fwd(j):
-        return same(xrows(j // ND, ry, cid_y(j % ND)), sy_send.at[j], sy_recv.at[j], sib)
+        return same(xrows(j // ND, ry, cid_y(j % ND)), sy_send.at[j // ND], sy_recv.at[j // ND], sib)
 
     def sz_fwd(j):
-        return same(xrows(j // ND, ry, cid_z(j % ND)), sz_send.at[j], sz_recv.at[j], sib)
+        return same(xrows(j // ND, ry, cid_z(j % ND)), sz_send.at[j // ND], sz_recv.at[j // ND], sib)
 
     def own_out(s):
         return same(xg.at[s, pl.ds(r * block, block), :], own_send.at[s], own_recv.at[s], sib)
 
-    n_steps = 2 * ND + LAG
-    comb_end = 10
-    first_end = ND + LAG
-
-    def relay(j):
-        @pl.when(j < 2 * ND)
-        def _():
-            y_out(j).wait()
-
-            @pl.when(j % ND < NR)
-            def _():
-                z_fwd(j).start()
-
+    def y_steps(a, b):
+        def body(j, _):
+            y_out(j).wait_recv()
+            z_fwd(j).start()
             sy_fwd(j).start()
-
-        jz = j - LAG
-
-        @pl.when(jnp.logical_and(jz >= 0, (jz + ND) % ND < NR))
-        def _():
-            z_fwd(jz).wait()
-            sz_fwd(jz).start()
-
-    def relays(a, b):
+            return 0
+
+        lax.fori_loop(a, b, body, 0)
+
+    def z_steps(a, b):
         def body(j, _):
-            relay(j)
+            z_fwd(j).wait_recv()
+            sz_fwd(j).start()
             return 0
 
         lax.fori_loop(a, b, body, 0)
+
+    def half_rows(s):
+        return xg.at[s, pl.ds(0, ND * ch), :]
+
+    def sib_waits(s):
+        same(half_rows(s), sy_send.at[s], sy_recv.at[s], sib).wait_recv()
+        same(half_rows(s), sz_send.at[s], sz_recv.at[s], sib).wait_recv()
+
+    def gather_sends_wait(s):
+        for send, recv, dev in ((y_send, own_recv, yn), (z_send, own_recv, zn), (sy_send, own_recv, sib),
+                                (sz_send, own_recv, sib)):
+            same(half_rows(s), send.at[s], recv.at[s], dev).wait_send()
 
     x_loads[0].wait()
     for j in range(ND):
@@ -266,15 +272,15 @@
         return ref.at[pl.ds(2 * k, 2)]
 
     def pre(idx):
-        return remote(half(l_buf.at[idx % 2], 1 - c), pre_buf.at[idx], pre_send.at[idx], pre_recv.at[idx], sib)
+        return remote(half(l_buf.at[idx % 2], 1 - c), pre_buf.at[idx], pre_send.at[idx - 2], pre_recv.at[idx - 2], sib)
 
     def bcast(idx, k):
         q = lax.rem(chip + k, n_chips)
-        return remote(bc_src.at[idx], bc_buf.at[idx, k - 1], bc_send.at[idx, k - 1], bc_recv.at[idx, k - 1],
+        return remote(bc_src.at[idx], bc_buf.at[idx, k - 1], bc_send.at[idx - 2], bc_recv.at[idx - 2],
                       {"comp": q // y_size, "row": (q % y_size) * CORES + c})
 
     def post(idx):
-        return same(half(tot_buf.at[idx], c), post_send.at[idx], post_recv.at[idx], sib)
+        return same(half(tot_buf.at[idx], c), post_send.at[idx - 2], post_recv.at[idx - 2], sib)
 
     def p2(idx):
         pre(idx).wait()
@@ -283,17 +289,16 @@
             bcast(idx, k).start()
 
     def p3(idx):
-        for k in range(1, n_chips):
-            bcast(idx, k).wait()
+        same(bc_buf.at[idx], bc_send.at[idx - 2], bc_recv.at[idx - 2], sib).wait()
         tot_buf[idx, pl.ds(2 * c, 2)] = lse2_parts([bc_src[idx]] + [bc_buf[idx, k] for k in range(n_chips - 1)])
         post(idx).start()
 
     def zl(s, k):
-        return remote(zl_src.at[s], zl_buf.at[s, k - 1], zl_send.at[s, k - 1], zl_recv.at[s, k - 1],
+        return remote(zl_src.at[s], zl_buf.at[s, k - 1], zl_send.at[s], zl_recv.at[s],
                       {"comp": lax.rem(z + k, comp_size)})
 
     def ag(s, k):
-        return same(tot_buf.at[s, r], ag_send.at[s, k], ag_recv.at[s, k], (sib, yn, yd)[k])
+        return same(tot_buf.at[s, r], ag_send.at[s], ag_recv.at[s], (sib, yn, yd)[k])
 
     def orig_fit(s, _):
         def orig_slots(p, _):
@@ -312,7 +317,7 @@
 
             @pl.when(s == 1)
             def _():
-                relays(2 * p, 2 * p + 2)
+                y_steps(1 + 2 * p, 3 + 2 * p)
 
             return 0
 
@@ -325,6 +330,11 @@
 
         for k in range(1, comp_size):
             zl(s, k).start()
+
+        @pl.when(s == 0)
+        def _():
+            y_steps(0, 1)
+
         return 0
 
     lax.fori_loop(0, 2, orig_fit, 0)
@@ -336,59 +346,47 @@
 
         lax.fori_loop(a, b, send, 0)
 
-    early = ND + 3
-    y_sends(ND, early)
-
-    def comb(s, _):
-        relays(4 + 3 * s, 7 + 3 * s)
-        for k in range(1, comp_size):
-            zl(s, k).wait()
+    def comb(s):
+        same(zl_buf.at[s], zl_send.at[s], zl_recv.at[s], sib).wait()
         tot_buf[s, r] = lse2_parts([zl_src[s]] + [zl_buf[s, k] for k in range(comp_size - 1)])
         for k in range(3):
             ag(s, k).start()
 
-        @pl.when(s == 0)
-        def _():
-            y_sends(early, 2 * ND)
-
-        return 0
-
-    lax.fori_loop(0, 2, comb, 0)
+    early = ND + 5
+    y_sends(ND, early)
+    y_steps(5, 6)
+    comb(0)
+    y_sends(early, 2 * ND)
+    y_steps(6, 8)
+    z_steps(0, 4)
+    y_steps(8, 9)
+    z_steps(4, 6)
+    y_steps(9, 10)
+    comb(1)
+    z_steps(6, 8)
+    y_steps(10, 12)
 
     def sweep0(s, _):
-        @pl.when(s == 0)
-        def _():
-            relays(comb_end, first_end)
-
-        for k in range(3):
-            ag(s, k).wait()
+        same(tot_buf.at[s, pl.ds(0, 3)], ag_send.at[s], ag_recv.at[s], sib).wait()
         own_out(s).wait()
         acc_zero()
 
-        def sib_waits(j, _):
-            sy_fwd(j).wait()
-
-            @pl.when(j % ND < NR)
-            def _():
-                sz_fwd(j).wait()
-
-            return 0
-
         @pl.when(s == 0)
         def _():
-            lax.fori_loop(0, ND, sib_waits, 0)
+            sib_waits(0)
 
         def body(k, _):
             @pl.when(jnp.logical_and(s == 1, k == 1))
             def _():
-                relays(first_end + 6, n_steps)
-                lax.fori_loop(ND, 2 * ND, sib_waits, 0)
+                z_steps(14, 16)
+                sib_waits(1)
 
             mr_half(s, r, 0, y + k * (1 - 2 * y))
 
             @pl.when(s == 0)
             def _():
-                relays(first_end + 2 * k, first_end + 2 * k + 2)
+                y_steps(12 + 2 * k, 14 + k)
+                z_steps(8 + k, 9 + 2 * k)
 
             return 0
 
@@ -399,12 +397,81 @@
         def hook(i):
             @pl.when(jnp.logical_and(s == 0, i == 0))
             def _():
-                relays(first_end + 4, first_end + 6)
+                y_steps(15, 16)
+                z_steps(11, 13)
 
         e_step(s, 1, 2 + s, hook)
+
+        @pl.when(s == 0)
+        def _():
+            z_steps(13, 14)
+
         return 0
 
     lax.fori_loop(0, 2, sweep0, 0)
+
+    def mx(s):
+        return same(mub.at[s, r], mx_send.at[s], mx_recv.at[s], yn)
+
+    def br(s):
+        return same(brow.at[s, r], br_send.at[s], br_recv.at[s], yn)
+
+    def mean_rows(slot, s):
+        return mu_out.at[s, pl.ds(pl.multiple_of(slot * n_own, n_own), n_own), :]
+
+    def fin(slot, s, k):
+        return same(mean_rows(slot, s), fin_send.at[s, k], fin_recv.at[s, k], sib)
+
+    def lpf(slot, k):
+        return same(lp_fin.at[slot], lpf_send.at[k], lpf_recv.at[k], sib)
+
+    def sweep(i, _):
+        t, s = i // 2, i % 2
+        last = t == sweeps - 1
+        p3(i)
+        m_step(s, t)
+        mean, logw = acc_result()
+
+        @pl.when(t < sweeps - 1)
+        def _():
+            col = set_params(s, r, mean, logw, t + 1)
+
+            @pl.when(t == sweeps - 2)
+            def _():
+                brow[s, r] = col_to_row(col)
+
+            e_step(s, t + 1, i + 2)
+
+            @pl.when(t == sweeps - 2)
+            def _():
+                mx(s).start()
+                br(s).start()
+
+        @pl.when(last)
+        def _():
+            mean_rows(r, s)[...] = mean
+            lp_fin[r, pl.ds(s, 1), :] = col_to_row(logw)
+            fin(r, s, 0).start()
+            mx(s).wait()
+            br(s).wait()
+            bcol[s, ry] = jnp.broadcast_to(row_to_col(brow[s, ry]), (n_own, 128))
+            acc_zero()
+
+            def body(h, _):
+                mr_half(s, ry, t, h)
+                return 0
+
+            lax.fori_loop(0, 2, body, 0)
+            mean2, logw2 = acc_result()
+            mean_rows(ry, s)[...] = mean2
+            lp_fin[ry, pl.ds(s, 1), :] = col_to_row(logw2)
+            fin(ry, s, 1).start()
+
+        return 0
+
+    lax.fori_loop(2, 2 * sweeps, sweep, 0)
+    lpf(r, 0).start()
+    lpf(ry, 1).start()
 
     ones = jnp.ones((8, half_dim), jnp.bfloat16)
 
@@ -419,68 +486,8 @@
 
     lax.fori_loop(0, 2, sq_norms, 0)
 
-    def mx(s):
-        return same(mub.at[s, r], mx_send.at[s], mx_recv.at[s], yn)
-
-    def br(s):
-        return same(brow.at[s, r], br_send.at[s], br_recv.at[s], yn)
-
-    def mean_rows(slot, s):
-        return mu_out.at[s, pl.ds(pl.multiple_of(slot * n_own, n_own), n_own), :]
-
-    def fin(slot, s, k):
-        return same(mean_rows(slot, s), fin_send.at[s, k], fin_recv.at[s, k], sib)
-
-    def lpf(slot, k):
-        return same(lp_fin.at[slot], lpf_send.at[k], lpf_recv.at[k], sib)
-
-    def sweep(i, _):
-        t, s = i // 2, i % 2
-        last = t == sweeps - 1
-        p3(i)
-        m_step(s, t)
-        mean, logw = acc_result()
-
-        @pl.when(t < sweeps - 1)
-        def _():
-            col = set_params(s, r, mean, logw, t + 1)
-
-            @pl.when(t == sweeps - 2)
-            def _():
-                brow[s, r] = col_to_row(col)
-
-            e_step(s, t + 1, i + 2)
-
-            @pl.when(t == sweeps - 2)
-            def _():
-                mx(s).start()
-                br(s).start()
-
-        @pl.when(last)
-        def _():
-            mean_rows(r, s)[...] = mean
-            lp_fin[r, pl.ds(s, 1), :] = col_to_row(logw)
-            fin(r, s, 0).start()
-            mx(s).wait()
-            br(s).wait()
-            bcol[s, ry] = jnp.broadcast_to(row_to_col(brow[s, ry]), (n_own, 128))
-            acc_zero()
-
-            def body(h, _):
-                mr_half(s, ry, t, h)
-                return 0
-
-            lax.fori_loop(0, 2, body, 0)
-            mean2, logw2 = acc_result()
-            mean_rows(ry, s)[...] = mean2
-            lp_fin[ry, pl.ds(s, 1), :] = col_to_row(logw2)
-            fin(ry, s, 1).start()
-
-        return 0
-
-    lax.fori_loop(2, 2 * sweeps, sweep, 0)
-    lpf(r, 0).start()
-    lpf(ry, 1).start()
+    for s in range(2):
+        gather_sends_wait(s)
 
     t = sweeps - 1
     for s in range(2):
@@ -536,15 +543,13 @@
             vm((ni, n_chips - 1, 2, bt, TP), f32),
             vm((ni, row_size, bt, TP), f32),
             dma((4,)), pltpu.SemaphoreType.REGULAR, pltpu.SemaphoreType.REGULAR,
-            dma((2 * ND,)), dma((2 * ND,)), dma((2 * ND,)), dma((2 * ND,)),
-            dma((2 * ND,)), dma((2 * ND,)), dma((2 * ND,)), dma((2 * ND,)),
-            dma((2,)), dma((2,)),
-            dma((2, comp_size - 1)), dma((2, comp_size - 1)), dma((2, 3)), dma((2, 3)),
-            dma((ni,)), dma((ni,)), dma((ni, n_chips - 1)), dma((ni, n_chips - 1)), dma((ni,)), dma((ni,)),
+            dma((2,)), dma((2 * ND,)), dma((2,)), dma((2 * ND,)), dma((2,)), dma((2,)), dma((2,)), dma((2,)),
+            dma((2,)), dma((2,)), dma((2,)), dma((2,)), dma((2,)), dma((2,)),
+            dma((ni - 2,)), dma((ni - 2,)), dma((ni - 2,)), dma((ni - 2,)), dma((ni - 2,)), dma((ni - 2,)),
             dma((2,)), dma((2,)), dma((2,)), dma((2,)),
             dma((2, 2)), dma((2, 2)), dma((2,)), dma((2,)),
         ]
-        return pl.pallas_call(
+        outs = pl.pallas_call(
             functools.partial(em_kernel, comp_size, row_size, sweeps),
             out_shape=(vm((2, n_local, half_dim), f32), vm((2, n_local), f32), vm((2, block), f32)),
             in_specs=[
@@ -558,6 +563,13 @@
             compiler_params=pltpu.CompilerParams(
                 collective_id=0, has_side_effects=True, vmem_limit_bytes=56 * 1024 * 1024),
         )(inv_temp, logpi_init, x_local, mu_init)
+        return pl.pallas_call(
+            write_kernel,
+            out_shape=tuple(jax.ShapeDtypeStruct(o.shape, o.dtype) for o in outs),
+            in_specs=[pl.BlockSpec(memory_space=pltpu.VMEM)] * 3,
+            out_specs=(pl.BlockSpec(memory_space=pl.ANY),) * 3,
+            scratch_shapes=[dma((3,))],
+        )(*[pltpu.with_memory_space_constraint(o, pltpu.VMEM) for o in outs])
 
     return jax.shard_map(
         local_fit,

time: 52.1 us -> 47.5 us (0.912)
  local copies, waits for them, and re-layouts: 2.52 us -> 0 us
  Pallas kernels: 48.7 us -> 46.6 us
    pallas_call x1, Pallas kernels: 48.7 us -> 45.2 us  [local_fit(): pl.pallas_call(functools.partial(em_kernel, comp_size, row_size, sweeps),...]
    unnamed x3 -> x0, local copies, waits for them, and re-layouts: 2.52 us -> none
    pallas_call x0 -> x1, Pallas kernels: none -> 1.35 us  [local_fit(): pl.pallas_call(write_kernel, out_shape=tuple((jax.ShapeDtypeStruct(o.shap...]
where the time goes in v5:
time: 47.5 us; the launch traced here: 47.2 us
  Pallas kernels  46.6 us (98%)
  between operations  0.64 us (1%)
    pallas_call x1, Pallas kernels, local_fit(): pl.pallas_call(functools.partial(em_kernel, comp_size, row_size, sweeps),...  45.2 us
    pallas_call x1, Pallas kernels, local_fit(): pl.pallas_call(write_kernel, out_shape=tuple((jax.ShapeDtypeStruct(o.shap...  1.35 us

profile of v5, /device:TPU:0, one launch (start us, length us, event | category | flops | bytes accessed | tf_op | source)
XLA Modules:
  0.0 47.2 jit_solution(3383947029407813989)
XLA Ops:
  0.6 45.2 %shard_map.67 = (f32[2,1024,256]{2,1,0:T(8,128)S(1)}, f32[2,1024]{1,0:T(2,128)S(1)}, f32[2,1024]{1,0:T(2,128)S(1)}) custom-call(f32[3]{0:T(128)} %temp_ref.1, f32[2,1024]{1,0:T(2,128)} %lp_ref.1, bf16[1024,512]{1,0:T(8,128)(2,1)} %x_hbm.1, f32[2,1024,256]{2,1,0:T(8,128)} %mu_hbm.1), custom_call_target="tpu_custom_call" | custom-call | tf_op jit(solution)/shard_map/pallas_call | solution.py:552
  45.9 1.4 %shard_map.68 = (f32[2,1024,256]{2,1,0:T(8,128)}, f32[2,1024]{1,0:T(2,128)}, f32[2,1024]{1,0:T(2,128)}) custom-call(f32[2,1024,256]{2,1,0:T(8,128)S(1)} %get-tuple-element.6.a, f32[2,1024]{1,0:T(2,128)S(1)} %get-tuple-element.7.b, f32[2,1024]{1,0:T(2,128)S(1)} %get-tuple-element.8.c), custom_call_target="tpu_custom_call" | custom-call | tf_op jit(solution)/shard_map/pallas_call | solution.py:566

commit v6 on v5

--- a/solution.py
+++ b/solution.py
@@ -96,7 +96,7 @@
         x_hbm.at[:, pl.ds(s * half_dim, half_dim)], xg.at[s, pl.ds(r * block, block), :], load_sem.at[s])
         for s in range(2)]
     mu_loads = [pltpu.make_async_copy(mu_hbm.at[s], mu_all.at[s], load_sem.at[2 + s]) for s in range(2)]
-    for cp in x_loads + mu_loads:
+    for cp in x_loads:
         cp.start()
 
     n_z = (z > 0).astype(jnp.int32) + (z < comp_size - 1).astype(jnp.int32)
@@ -119,6 +119,8 @@
     signal_near(barrier)
     pl.semaphore_wait(barrier, 2 + n_z)
     signal_near(near_sem)
+    for cp in mu_loads:
+        cp.start()
 
     def xrows(s, blk, cid):
         return xg.at[s, pl.ds(pl.multiple_of(blk * block + cid * ch, ch), ch), :]
@@ -261,6 +263,10 @@
             return jnp.exp2(a * (temp_ref[t] * (2.0 * LOG2E)) + twice(bcol[s, slot]) - tot_buf[idx, b, u:u + 1, :])
 
         acc_tiles(s, tiles_of(half_id), resp_of)
+
+    def mr_all(s, slot, t):
+        for h in range(2):
+            mr_half(s, slot, t, h)
 
     def acc_result():
         cnt = jnp.sum(n_acc[...], axis=1, keepdims=True)
@@ -352,7 +358,7 @@
         for k in range(3):
             ag(s, k).start()
 
-    early = ND + 5
+    early = ND + 3
     y_sends(ND, early)
     y_steps(5, 6)
     comb(0)
@@ -366,113 +372,6 @@
     z_steps(6, 8)
     y_steps(10, 12)
 
-    def sweep0(s, _):
-        same(tot_buf.at[s, pl.ds(0, 3)], ag_send.at[s], ag_recv.at[s], sib).wait()
-        own_out(s).wait()
-        acc_zero()
-
-        @pl.when(s == 0)
-        def _():
-            sib_waits(0)
-
-        def body(k, _):
-            @pl.when(jnp.logical_and(s == 1, k == 1))
-            def _():
-                z_steps(14, 16)
-                sib_waits(1)
-
-            mr_half(s, r, 0, y + k * (1 - 2 * y))
-
-            @pl.when(s == 0)
-            def _():
-                y_steps(12 + 2 * k, 14 + k)
-                z_steps(8 + k, 9 + 2 * k)
-
-            return 0
-
-        lax.fori_loop(0, 2, body, 0)
-        mean, logw = acc_result()
-        set_params(s, r, mean, logw, 1)
-
-        def hook(i):
-            @pl.when(jnp.logical_and(s == 0, i == 0))
-            def _():
-                y_steps(15, 16)
-                z_steps(11, 13)
-
-        e_step(s, 1, 2 + s, hook)
-
-        @pl.when(s == 0)
-        def _():
-            z_steps(13, 14)
-
-        return 0
-
-    lax.fori_loop(0, 2, sweep0, 0)
-
-    def mx(s):
-        return same(mub.at[s, r], mx_send.at[s], mx_recv.at[s], yn)
-
-    def br(s):
-        return same(brow.at[s, r], br_send.at[s], br_recv.at[s], yn)
-
-    def mean_rows(slot, s):
-        return mu_out.at[s, pl.ds(pl.multiple_of(slot * n_own, n_own), n_own), :]
-
-    def fin(slot, s, k):
-        return same(mean_rows(slot, s), fin_send.at[s, k], fin_recv.at[s, k], sib)
-
-    def lpf(slot, k):
-        return same(lp_fin.at[slot], lpf_send.at[k], lpf_recv.at[k], sib)
-
-    def sweep(i, _):
-        t, s = i // 2, i % 2
-        last = t == sweeps - 1
-        p3(i)
-        m_step(s, t)
-        mean, logw = acc_result()
-
-        @pl.when(t < sweeps - 1)
-        def _():
-            col = set_params(s, r, mean, logw, t + 1)
-
-            @pl.when(t == sweeps - 2)
-            def _():
-                brow[s, r] = col_to_row(col)
-
-            e_step(s, t + 1, i + 2)
-
-            @pl.when(t == sweeps - 2)
-            def _():
-                mx(s).start()
-                br(s).start()
-
-        @pl.when(last)
-        def _():
-            mean_rows(r, s)[...] = mean
-            lp_fin[r, pl.ds(s, 1), :] = col_to_row(logw)
-            fin(r, s, 0).start()
-            mx(s).wait()
-            br(s).wait()
-            bcol[s, ry] = jnp.broadcast_to(row_to_col(brow[s, ry]), (n_own, 128))
-            acc_zero()
-
-            def body(h, _):
-                mr_half(s, ry, t, h)
-                return 0
-
-            lax.fori_loop(0, 2, body, 0)
-            mean2, logw2 = acc_result()
-            mean_rows(ry, s)[...] = mean2
-            lp_fin[ry, pl.ds(s, 1), :] = col_to_row(logw2)
-            fin(ry, s, 1).start()
-
-        return 0
-
-    lax.fori_loop(2, 2 * sweeps, sweep, 0)
-    lpf(r, 0).start()
-    lpf(ry, 1).start()
-
     ones = jnp.ones((8, half_dim), jnp.bfloat16)
 
     def sq_norms(s, _):
@@ -484,7 +383,109 @@
             sq_buf[s, u:u + 1, :] = (dot_t(ones, hi) + dot_t(ones, lo))[0:1]
         return 0
 
-    lax.fori_loop(0, 2, sq_norms, 0)
+    def sweep0(s, _):
+        same(tot_buf.at[s, pl.ds(0, 3)], ag_send.at[s], ag_recv.at[s], sib).wait()
+        own_out(s).wait()
+        acc_zero()
+
+        @pl.when(s == 0)
+        def _():
+            sib_waits(0)
+            y_steps(12, 14)
+
+        def body(k, _):
+            @pl.when(jnp.logical_and(s == 1, k == 1))
+            def _():
+                z_steps(15, 16)
+                lax.fori_loop(0, 2, sq_norms, 0)
+                sib_waits(1)
+
+            mr_half(s, r, 0, y + k * (1 - 2 * y))
+
+            @pl.when(s == 0)
+            def _():
+                y_steps(14 + k, 15 + k)
+                z_steps(8 + 2 * k, 10 + k)
+
+            return 0
+
+        lax.fori_loop(0, 2, body, 0)
+        mean, logw = acc_result()
+        set_params(s, r, mean, logw, 1)
+
+        def hook(i):
+            @pl.when(jnp.logical_and(s == 0, i == 0))
+            def _():
+                z_steps(11, 13)
+
+        e_step(s, 1, 2 + s, hook)
+
+        @pl.when(s == 0)
+        def _():
+            z_steps(13, 15)
+
+        return 0
+
+    lax.fori_loop(0, 2, sweep0, 0)
+
+    def mx(s):
+        return same(mub.at[s, r], mx_send.at[s], mx_recv.at[s], yn)
+
+    def br(s):
+        return same(brow.at[s, r], br_send.at[s], br_recv.at[s], yn)
+
+    def mean_rows(slot, s):
+        return mu_out.at[s, pl.ds(pl.multiple_of(slot * n_own, n_own), n_own), :]
+
+    def fin(slot, s, k):
+        return same(mean_rows(slot, s), fin_send.at[s, k], fin_recv.at[s, k], sib)
+
+    def lpf(slot, k):
+        return same(lp_fin.at[slot], lpf_send.at[k], lpf_recv.at[k], sib)
+
+    def sweep(i, _):
+        t, s = i // 2, i % 2
+        last = t == sweeps - 1
+        p3(i)
+        m_step(s, t)
+        mean, logw = acc_result()
+
+        @pl.when(t < sweeps - 1)
+        def _():
+            col = set_params(s, r, mean, logw, t + 1)
+
+            @pl.when(t == sweeps - 2)
+            def _():
+                brow[s, r] = col_to_row(col)
+
+            e_step(s, t + 1, i + 2)
+
+            @pl.when(t == sweeps - 2)
+            def _():
+                mx(s).start()
+                br(s).start()
+
+        @pl.when(last)
+        def _():
+            mean_rows(r, s)[...] = mean
+            lp_fin[r, pl.ds(s, 1), :] = col_to_row(logw)
+            fin(r, s, 0).start()
+            mx(s).wait()
+            br(s).wait()
+            bcol[s, ry] = jnp.broadcast_to(row_to_col(brow[s, ry]), (n_own, 128))
+            acc_zero()
+
+            mr_all(s, ry, t)
+            mean2, logw2 = acc_result()
+            mean_rows(ry, s)[...] = mean2
+            lp_fin[ry, pl.ds(s, 1), :] = col_to_row(logw2)
+            fin(ry, s, 1).start()
+
+        return 0
+
+    lax.fori_loop(2, 2 * sweeps, sweep, 0)
+    lpf(r, 0).start()
+    lpf(ry, 1).start()
 
     for s in range(2):
         gather_sends_wait(s)

time: 47.5 us -> 46.7 us (0.983)
  Pallas kernels: 46.6 us -> 45.8 us
    pallas_call x1, Pallas kernels: 45.2 us -> 44.5 us  [local_fit(): pl.pallas_call(functools.partial(em_kernel, comp_size, row_size, sweeps),...]
where the time goes in v6:
time: 46.7 us; the launch traced here: 46.4 us
  Pallas kernels  45.8 us (98%)
  between operations  0.64 us (1%)
    pallas_call x1, Pallas kernels, local_fit(): pl.pallas_call(functools.partial(em_kernel, comp_size, row_size, sweeps),...  44.5 us
    pallas_call x1, Pallas kernels, local_fit(): pl.pallas_call(write_kernel, out_shape=tuple((jax.ShapeDtypeStruct(o.shap...  1.35 us

profile of v6, /device:TPU:0, one launch (start us, length us, event | category | flops | bytes accessed | tf_op | source)
XLA Modules:
  0.0 46.4 jit_solution(12355183053117464398)
XLA Ops:
  0.6 44.5 %shard_map.67 = (f32[2,1024,256]{2,1,0:T(8,128)S(1)}, f32[2,1024]{1,0:T(2,128)S(1)}, f32[2,1024]{1,0:T(2,128)S(1)}) custom-call(f32[3]{0:T(128)} %temp_ref.1, f32[2,1024]{1,0:T(2,128)} %lp_ref.1, bf16[1024,512]{1,0:T(8,128)(2,1)} %x_hbm.1, f32[2,1024,256]{2,1,0:T(8,128)} %mu_hbm.1), custom_call_target="tpu_custom_call" | custom-call | tf_op jit(solution)/shard_map/pallas_call | solution.py:553
  45.1 1.4 %shard_map.68 = (f32[2,1024,256]{2,1,0:T(8,128)}, f32[2,1024]{1,0:T(2,128)}, f32[2,1024]{1,0:T(2,128)}) custom-call(f32[2,1024,256]{2,1,0:T(8,128)S(1)} %get-tuple-element.6.a, f32[2,1024]{1,0:T(2,128)S(1)} %get-tuple-element.7.b, f32[2,1024]{1,0:T(2,128)S(1)} %get-tuple-element.8.c), custom_call_target="tpu_custom_call" | custom-call | tf_op jit(solution)/shard_map/pallas_call | solution.py:567

commit v7 on v6

--- a/solution.py
+++ b/solution.py
@@ -55,11 +55,11 @@
 
 def em_kernel(
     comp_size, row_size, sweeps,
-    temp_ref, lp_ref, x_hbm, mu_hbm,
+    temp_hbm, lp_hbm, x_hbm, mu_hbm,
     mu_out, lp_out, lse_out,
-    xg, mu_all, mub, bcol, brow, e_buf, m_buf, l_buf, lq_buf, s_acc, n_acc, lp_fin, sq_buf,
+    temp_ref, lp_ref, xg, mu_all, mub, bcol, brow, e_buf, m_buf, l_buf, lq_buf, s_acc, n_acc, lp_fin, sq_buf,
     zl_src, zl_buf, pre_buf, bc_src, bc_buf, tot_buf,
-    load_sem, near_sem, far_sem, y_send, y_recv, z_send, z_recv, sy_send, sy_recv, sz_send, sz_recv, own_send, own_recv,
+    load_sem, near_sem, far_sem, g_send, y_recv, z_recv, sy_recv, sz_recv, own_recv,
     zl_send, zl_recv, ag_send, ag_recv,
     pre_send, pre_recv, bc_send, bc_recv, post_send, post_recv,
     mx_send, mx_recv, br_send, br_recv, fin_send, fin_recv, lpf_send, lpf_recv,
@@ -96,7 +96,9 @@
         x_hbm.at[:, pl.ds(s * half_dim, half_dim)], xg.at[s, pl.ds(r * block, block), :], load_sem.at[s])
         for s in range(2)]
     mu_loads = [pltpu.make_async_copy(mu_hbm.at[s], mu_all.at[s], load_sem.at[2 + s]) for s in range(2)]
-    for cp in x_loads:
+    small_loads = [pltpu.make_async_copy(temp_hbm, temp_ref, load_sem.at[4]),
+                   pltpu.make_async_copy(lp_hbm, lp_ref, load_sem.at[5])]
+    for cp in x_loads + small_loads:
         cp.start()
 
     n_z = (z > 0).astype(jnp.int32) + (z < comp_size - 1).astype(jnp.int32)
@@ -132,19 +134,19 @@
         return k + (1 - hz) * (NCK - 1 - 2 * k)
 
     def y_out(j):
-        return same(xrows(j // ND, r, cid_y(j % ND)), y_send.at[j // ND], y_recv.at[j], yn)
+        return same(xrows(j // ND, r, cid_y(j % ND)), g_send.at[0], y_recv.at[j], yn)
 
     def z_fwd(j):
-        return same(xrows(j // ND, ry, cid_y(j % ND)), z_send.at[j // ND], z_recv.at[j], zn)
+        return same(xrows(j // ND, ry, cid_y(j % ND)), g_send.at[0], z_recv.at[j], zn)
 
     def sy_fwd(j):
-        return same(xrows(j // ND, ry, cid_y(j % ND)), sy_send.at[j // ND], sy_recv.at[j // ND], sib)
+        return same(xrows(j // ND, ry, cid_y(j % ND)), g_send.at[0], sy_recv.at[j // ND], sib)
 
     def sz_fwd(j):
-        return same(xrows(j // ND, ry, cid_z(j % ND)), sz_send.at[j // ND], sz_recv.at[j // ND], sib)
+        return same(xrows(j // ND, ry, cid_z(j % ND)), g_send.at[0], sz_recv.at[j // ND], sib)
 
     def own_out(s):
-        return same(xg.at[s, pl.ds(r * block, block), :], own_send.at[s], own_recv.at[s], sib)
+        return same(xg.at[s, pl.ds(r * block, block), :], g_send.at[0], own_recv.at[s], sib)
 
     def y_steps(a, b):
         def body(j, _):
@@ -167,13 +169,13 @@
         return xg.at[s, pl.ds(0, ND * ch), :]
 
     def sib_waits(s):
-        same(half_rows(s), sy_send.at[s], sy_recv.at[s], sib).wait_recv()
-        same(half_rows(s), sz_send.at[s], sz_recv.at[s], sib).wait_recv()
+        same(half_rows(s), g_send.at[0], sy_recv.at[s], sib).wait_recv()
+        same(half_rows(s), g_send.at[0], sz_recv.at[s], sib).wait_recv()
 
     def gather_sends_wait(s):
-        for send, recv, dev in ((y_send, own_recv, yn), (z_send, own_recv, zn), (sy_send, own_recv, sib),
-                                (sz_send, own_recv, sib)):
-            same(half_rows(s), send.at[s], recv.at[s], dev).wait_send()
+        for _ in range(4):
+            same(half_rows(s), g_send.at[0], sy_recv.at[s], sib).wait_send()
+        own_out(s).wait_send()
 
     x_loads[0].wait()
     for j in range(ND):
@@ -181,7 +183,7 @@
     own_out(0).start()
     x_loads[1].wait()
     own_out(1).start()
-    for cp in mu_loads:
+    for cp in mu_loads + small_loads:
         cp.wait()
 
     def set_params(s, slot, mean, logw, t):
@@ -270,7 +272,7 @@
 
     def acc_result():
         cnt = jnp.sum(n_acc[...], axis=1, keepdims=True)
-        mean = s_acc[...] / (cnt + EPS_COUNT)
+        mean = s_acc[...] * (1.0 / (cnt + EPS_COUNT))
         logw = jnp.log((cnt + PRIOR_ALPHA) / (total_pts + total_comp * PRIOR_ALPHA))
         return mean, logw
 
@@ -280,7 +282,8 @@
     def pre(idx):
         return remote(half(l_buf.at[idx % 2], 1 - c), pre_buf.at[idx], pre_send.at[idx - 2], pre_recv.at[idx - 2], sib)
 
-    def bcast(idx, k):
+    def bcast(idx, j):
+        k = jnp.where(z < comp_size // 2, n_chips - j, j)
         q = lax.rem(chip + k, n_chips)
         return remote(bc_src.at[idx], bc_buf.at[idx, k - 1], bc_send.at[idx - 2], bc_recv.at[idx - 2],
                       {"comp": q // y_size, "row": (q % y_size) * CORES + c})
@@ -385,18 +388,17 @@
 
     def sweep0(s, _):
         same(tot_buf.at[s, pl.ds(0, 3)], ag_send.at[s], ag_recv.at[s], sib).wait()
-        own_out(s).wait()
+        own_out(s).wait_recv()
         acc_zero()
 
         @pl.when(s == 0)
         def _():
             sib_waits(0)
-            y_steps(12, 14)
+            y_steps(12, 15)
 
         def body(k, _):
             @pl.when(jnp.logical_and(s == 1, k == 1))
             def _():
-                z_steps(15, 16)
                 lax.fori_loop(0, 2, sq_norms, 0)
                 sib_waits(1)
 
@@ -404,8 +406,8 @@
 
             @pl.when(s == 0)
             def _():
-                y_steps(14 + k, 15 + k)
-                z_steps(8 + 2 * k, 10 + k)
+                y_steps(15, 16 - k)
+                z_steps(8 + 3 * k, 11 + 2 * k)
 
             return 0
 
@@ -416,13 +418,13 @@
         def hook(i):
             @pl.when(jnp.logical_and(s == 0, i == 0))
             def _():
-                z_steps(11, 13)
+                z_steps(13, 15)
 
         e_step(s, 1, 2 + s, hook)
 
         @pl.when(s == 0)
         def _():
-            z_steps(13, 15)
+            z_steps(15, 16)
 
         return 0
 
@@ -524,6 +526,7 @@
         dma = pltpu.SemaphoreType.DMA
         vm = pltpu.VMEM
         scratch = [
+            pltpu.SMEM((sweeps,), f32), vm((2, n_local), f32),
             vm((2, total_pts, half_dim), bf16),
             vm((2, n_local, half_dim), f32),
             vm((2, row_size, n_own, half_dim), bf16),
@@ -543,9 +546,9 @@
             vm((ni, 2, bt, TP), f32),
             vm((ni, n_chips - 1, 2, bt, TP), f32),
             vm((ni, row_size, bt, TP), f32),
-            dma((4,)), pltpu.SemaphoreType.REGULAR, pltpu.SemaphoreType.REGULAR,
-            dma((2,)), dma((2 * ND,)), dma((2,)), dma((2 * ND,)), dma((2,)), dma((2,)), dma((2,)), dma((2,)),
-            dma((2,)), dma((2,)), dma((2,)), dma((2,)), dma((2,)), dma((2,)),
+            dma((6,)), pltpu.SemaphoreType.REGULAR, pltpu.SemaphoreType.REGULAR,
+            dma((1,)), dma((2 * ND,)), dma((2 * ND,)), dma((2,)), dma((2,)), dma((2,)),
+            dma((2,)), dma((2,)), dma((2,)), dma((2,)),
             dma((ni - 2,)), dma((ni - 2,)), dma((ni - 2,)), dma((ni - 2,)), dma((ni - 2,)), dma((ni - 2,)),
             dma((2,)), dma((2,)), dma((2,)), dma((2,)),
             dma((2, 2)), dma((2, 2)), dma((2,)), dma((2,)),
@@ -554,11 +557,8 @@
             functools.partial(em_kernel, comp_size, row_size, sweeps),
             out_shape=(vm((2, n_local, half_dim), f32), vm((2, n_local), f32), vm((2, block), f32)),
             in_specs=[
-                pl.BlockSpec(memory_space=pltpu.SMEM),
-                pl.BlockSpec(memory_space=pltpu.VMEM),
                 pl.BlockSpec(memory_space=pl.ANY),
-                pl.BlockSpec(memory_space=pl.ANY),
-            ],
+            ] * 4,
             out_specs=(pl.BlockSpec(memory_space=pltpu.VMEM),) * 3,
             scratch_shapes=scratch,
             compiler_params=pltpu.CompilerParams(

time: 46.7 us -> 46.6 us (level)
  no operation moved by 1% of the time
where the time goes in v7:
time: 46.6 us; the launch traced here: 46.5 us
  Pallas kernels  45.9 us (98%)
  between operations  0.64 us (1%)
    pallas_call x1, Pallas kernels, local_fit(): pl.pallas_call(functools.partial(em_kernel, comp_size, row_size, sweeps),...  44.5 us
    pallas_call x1, Pallas kernels, local_fit(): pl.pallas_call(write_kernel, out_shape=tuple((jax.ShapeDtypeStruct(o.shap...  1.35 us

profile of v7, /device:TPU:0, one launch (start us, length us, event | category | flops | bytes accessed | tf_op | source)
XLA Modules:
  0.0 46.5 jit_solution(10192235988310094025)
XLA Ops:
  0.6 44.5 %shard_map.67 = (f32[2,1024,256]{2,1,0:T(8,128)S(1)}, f32[2,1024]{1,0:T(2,128)S(1)}, f32[2,1024]{1,0:T(2,128)S(1)}) custom-call(f32[3]{0:T(128)} %temp_hbm.1, f32[2,1024]{1,0:T(2,128)} %lp_hbm.1, bf16[1024,512]{1,0:T(8,128)(2,1)} %x_hbm.1, f32[2,1024,256]{2,1,0:T(8,128)} %mu_hbm.1), custom_call_target="tpu_custom_call" | custom-call | tf_op jit(solution)/shard_map/pallas_call | solution.py:556
  45.1 1.4 %shard_map.68 = (f32[2,1024,256]{2,1,0:T(8,128)}, f32[2,1024]{1,0:T(2,128)}, f32[2,1024]{1,0:T(2,128)}) custom-call(f32[2,1024,256]{2,1,0:T(8,128)S(1)} %get-tuple-element.6.a, f32[2,1024]{1,0:T(2,128)S(1)} %get-tuple-element.7.b, f32[2,1024]{1,0:T(2,128)S(1)} %get-tuple-element.8.c), custom_call_target="tpu_custom_call" | custom-call | tf_op jit(solution)/shard_map/pallas_call | solution.py:567

commit v8 on v7

--- a/solution.py
+++ b/solution.py
@@ -375,6 +375,109 @@
     z_steps(6, 8)
     y_steps(10, 12)
 
+    def sweep0(s, _):
+        same(tot_buf.at[s, pl.ds(0, 3)], ag_send.at[s], ag_recv.at[s], sib).wait()
+        own_out(s).wait_recv()
+        acc_zero()
+
+        @pl.when(s == 0)
+        def _():
+            sib_waits(0)
+            y_steps(12, 15)
+
+        def body(k, _):
+            @pl.when(jnp.logical_and(s == 1, k == 1))
+            def _():
+                z_steps(15, 16)
+                sib_waits(1)
+
+            mr_half(s, r, 0, y + k * (1 - 2 * y))
+
+            @pl.when(s == 0)
+            def _():
+                y_steps(16 - k, 16)
+                z_steps(8 + 3 * k, 11 + k)
+
+            return 0
+
+        lax.fori_loop(0, 2, body, 0)
+        mean, logw = acc_result()
+        set_params(s, r, mean, logw, 1)
+
+        def hook(i):
+            @pl.when(jnp.logical_and(s == 0, i == 0))
+            def _():
+                z_steps(12, 14)
+
+        e_step(s, 1, 2 + s, hook)
+
+        @pl.when(s == 0)
+        def _():
+            z_steps(14, 15)
+
+        return 0
+
+    lax.fori_loop(0, 2, sweep0, 0)
+
+    def mx(s):
+        return same(mub.at[s, r], mx_send.at[s], mx_recv.at[s], yn)
+
+    def br(s):
+        return same(brow.at[s, r], br_send.at[s], br_recv.at[s], yn)
+
+    def mean_rows(slot, s):
+        return mu_out.at[s, pl.ds(pl.multiple_of(slot * n_own, n_own), n_own), :]
+
+    def fin(slot, s, k):
+        return same(mean_rows(slot, s), fin_send.at[s, k], fin_recv.at[s, k], sib)
+
+    def lpf(slot, k):
+        return same(lp_fin.at[slot], lpf_send.at[k], lpf_recv.at[k], sib)
+
+    def sweep(i, _):
+        t, s = i // 2, i % 2
+        last = t == sweeps - 1
+        p3(i)
+        m_step(s, t)
+        mean, logw = acc_result()
+
+        @pl.when(t < sweeps - 1)
+        def _():
+            col = set_params(s, r, mean, logw, t + 1)
+
+            @pl.when(t == sweeps - 2)
+            def _():
+                brow[s, r] = col_to_row(col)
+
+            e_step(s, t + 1, i + 2)
+
+            @pl.when(t == sweeps - 2)
+            def _():
+                mx(s).start()
+                br(s).start()
+
+        @pl.when(last)
+        def _():
+            mean_rows(r, s)[...] = mean
+            lp_fin[r, pl.ds(s, 1), :] = col_to_row(logw)
+            fin(r, s, 0).start()
+            mx(s).wait()
+            br(s).wait()
+            bcol[s, ry] = jnp.broadcast_to(row_to_col(brow[s, ry]), (n_own, 128))
+            acc_zero()
+
+            mr_all(s, ry, t)
+            mean2, logw2 = acc_result()
+            mean_rows(ry, s)[...] = mean2
+            lp_fin[ry, pl.ds(s, 1), :] = col_to_row(logw2)
+            fin(ry, s, 1).start()
+
+        return 0
+
+    lax.fori_loop(2, 2 * sweeps, sweep, 0)
+    lpf(r, 0).start()
+    lpf(ry, 1).start()
+
     ones = jnp.ones((8, half_dim), jnp.bfloat16)
 
     def sq_norms(s, _):
@@ -386,109 +489,7 @@
             sq_buf[s, u:u + 1, :] = (dot_t(ones, hi) + dot_t(ones, lo))[0:1]
         return 0
 
-    def sweep0(s, _):
-        same(tot_buf.at[s, pl.ds(0, 3)], ag_send.at[s], ag_recv.at[s], sib).wait()
-        own_out(s).wait_recv()
-        acc_zero()
-
-        @pl.when(s == 0)
-        def _():
-            sib_waits(0)
-            y_steps(12, 15)
-
-        def body(k, _):
-            @pl.when(jnp.logical_and(s == 1, k == 1))
-            def _():
-                lax.fori_loop(0, 2, sq_norms, 0)
-                sib_waits(1)
-
-            mr_half(s, r, 0, y + k * (1 - 2 * y))
-
-            @pl.when(s == 0)
-            def _():
-                y_steps(15, 16 - k)
-                z_steps(8 + 3 * k, 11 + 2 * k)
-
-            return 0
-
-        lax.fori_loop(0, 2, body, 0)
-        mean, logw = acc_result()
-        set_params(s, r, mean, logw, 1)
-
-        def hook(i):
-            @pl.when(jnp.logical_and(s == 0, i == 0))
-            def _():
-                z_steps(13, 15)
-
-        e_step(s, 1, 2 + s, hook)
-
-        @pl.when(s == 0)
-        def _():
-            z_steps(15, 16)
-
-        return 0
-
-    lax.fori_loop(0, 2, sweep0, 0)
-
-    def mx(s):
-        return same(mub.at[s, r], mx_send.at[s], mx_recv.at[s], yn)
-
-    def br(s):
-        return same(brow.at[s, r], br_send.at[s], br_recv.at[s], yn)
-
-    def mean_rows(slot, s):
-        return mu_out.at[s, pl.ds(pl.multiple_of(slot * n_own, n_own), n_own), :]
-
-    def fin(slot, s, k):
-        return same(mean_rows(slot, s), fin_send.at[s, k], fin_recv.at[s, k], sib)
-
-    def lpf(slot, k):
-        return same(lp_fin.at[slot], lpf_send.at[k], lpf_recv.at[k], sib)
-
-    def sweep(i, _):
-        t, s = i // 2, i % 2
-        last = t == sweeps - 1
-        p3(i)
-        m_step(s, t)
-        mean, logw = acc_result()
-
-        @pl.when(t < sweeps - 1)
-        def _():
-            col = set_params(s, r, mean, logw, t + 1)
-
-            @pl.when(t == sweeps - 2)
-            def _():
-                brow[s, r] = col_to_row(col)
-
-            e_step(s, t + 1, i + 2)
-
-            @pl.when(t == sweeps - 2)
-            def _():
-                mx(s).start()
-                br(s).start()
-
-        @pl.when(last)
-        def _():
-            mean_rows(r, s)[...] = mean
-            lp_fin[r, pl.ds(s, 1), :] = col_to_row(logw)
-            fin(r, s, 0).start()
-            mx(s).wait()
-            br(s).wait()
-            bcol[s, ry] = jnp.broadcast_to(row_to_col(brow[s, ry]), (n_own, 128))
-            acc_zero()
-
-            mr_all(s, ry, t)
-            mean2, logw2 = acc_result()
-            mean_rows(ry, s)[...] = mean2
-            lp_fin[ry, pl.ds(s, 1), :] = col_to_row(logw2)
-            fin(ry, s, 1).start()
-
-        return 0
-
-    lax.fori_loop(2, 2 * sweeps, sweep, 0)
-    lpf(r, 0).start()
-    lpf(ry, 1).start()
-
+    lax.fori_loop(0, 2, sq_norms, 0)
     for s in range(2):
         gather_sends_wait(s)
 

time: 46.6 us -> 46.2 us (level)
  Pallas kernels: 45.9 us -> 45.4 us
where the time goes in v8:
time: 46.2 us; the launch traced here: 46 us
  Pallas kernels  45.4 us (98%)
  between operations  0.64 us (1%)
    pallas_call x1, Pallas kernels, local_fit(): pl.pallas_call(functools.partial(em_kernel, comp_size, row_size, sweeps),...  44 us
    pallas_call x1, Pallas kernels, local_fit(): pl.pallas_call(write_kernel, out_shape=tuple((jax.ShapeDtypeStruct(o.shap...  1.35 us

profile of v8, /device:TPU:0, one launch (start us, length us, event | category | flops | bytes accessed | tf_op | source)
XLA Modules:
  0.0 46.0 jit_solution(16152000412857937535)
XLA Ops:
  0.6 44.0 %shard_map.67 = (f32[2,1024,256]{2,1,0:T(8,128)S(1)}, f32[2,1024]{1,0:T(2,128)S(1)}, f32[2,1024]{1,0:T(2,128)S(1)}) custom-call(f32[3]{0:T(128)} %temp_hbm.1, f32[2,1024]{1,0:T(2,128)} %lp_hbm.1, bf16[1024,512]{1,0:T(8,128)(2,1)} %x_hbm.1, f32[2,1024,256]{2,1,0:T(8,128)} %mu_hbm.1), custom_call_target="tpu_custom_call" | custom-call | tf_op jit(solution)/shard_map/pallas_call | solution.py:557
  44.7 1.4 %shard_map.68 = (f32[2,1024,256]{2,1,0:T(8,128)}, f32[2,1024]{1,0:T(2,128)}, f32[2,1024]{1,0:T(2,128)}) custom-call(f32[2,1024,256]{2,1,0:T(8,128)S(1)} %get-tuple-element.6.a, f32[2,1024]{1,0:T(2,128)S(1)} %get-tuple-element.7.b, f32[2,1024]{1,0:T(2,128)S(1)} %get-tuple-element.8.c), custom_call_target="tpu_custom_call" | custom-call | tf_op jit(solution)/shard_map/pallas_call | solution.py:568

commit v9 on v8

--- a/solution.py
+++ b/solution.py
@@ -81,8 +81,9 @@
     ry = (1 - y) * CORES + c
     sib = {"row": rs}
     yn = {"row": ry}
-    yd = {"row": (1 - y) * CORES + (1 - c)}
-    zn = {"comp": z + 1 - 2 * (z % 2)}
+    rx = (1 - y) * CORES + (1 - c)
+    yd = {"row": rx}
+    zx = {"comp": z + 1 - 2 * (z % 2), "row": rs}
     hz = z % 2
 
     def remote(src, dst, send, recv, dev):
@@ -113,13 +114,13 @@
             pl.semaphore_signal(sem, inc=1, device_id={"comp": z + 1}, device_id_type=MESH)
 
     def signal_near(sem):
-        for dev in (sib, yn):
+        for dev in (sib, yn, yd):
             pl.semaphore_signal(sem, inc=1, device_id=dev, device_id_type=MESH)
         signal_z(sem)
 
     barrier = pltpu.get_barrier_semaphore()
     signal_near(barrier)
-    pl.semaphore_wait(barrier, 2 + n_z)
+    pl.semaphore_wait(barrier, 3 + n_z)
     signal_near(near_sem)
     for cp in mu_loads:
         cp.start()
@@ -134,13 +135,13 @@
         return k + (1 - hz) * (NCK - 1 - 2 * k)
 
     def y_out(j):
-        return same(xrows(j // ND, r, cid_y(j % ND)), g_send.at[0], y_recv.at[j], yn)
+        return same(xrows(j // ND, r, cid_y(j % ND)), g_send.at[0], y_recv.at[j], yd)
 
     def z_fwd(j):
-        return same(xrows(j // ND, ry, cid_y(j % ND)), g_send.at[0], z_recv.at[j], zn)
+        return same(xrows(j // ND, rx, cid_y(j % ND)), g_send.at[0], z_recv.at[j], zx)
 
     def sy_fwd(j):
-        return same(xrows(j // ND, ry, cid_y(j % ND)), g_send.at[0], sy_recv.at[j // ND], sib)
+        return same(xrows(j // ND, rx, cid_y(j % ND)), g_send.at[0], sy_recv.at[j // ND], sib)
 
     def sz_fwd(j):
         return same(xrows(j // ND, ry, cid_z(j % ND)), g_send.at[0], sz_recv.at[j // ND], sib)
@@ -252,7 +253,7 @@
                 f = jnp.exp2(m_buf[s, b, u:u + 1, :] - tot_buf[idx, b, u:u + 1, :])
                 return e_buf[s, b * bt + u] * f
 
-            acc_tiles(s, tiles_of(c + i * (1 - 2 * c)), resp_of)
+            acc_tiles(s, tiles_of((1 - c) + i * (2 * c - 1)), resp_of)
             return 0
 
         lax.fori_loop(0, 2, body, 0)
@@ -283,23 +284,23 @@
         return remote(half(l_buf.at[idx % 2], 1 - c), pre_buf.at[idx], pre_send.at[idx - 2], pre_recv.at[idx - 2], sib)
 
     def bcast(idx, j):
-        k = jnp.where(z < comp_size // 2, n_chips - j, j)
+        k = lax.rem(jnp.where(z < comp_size // 2, n_chips - j, j), n_chips)
         q = lax.rem(chip + k, n_chips)
-        return remote(bc_src.at[idx], bc_buf.at[idx, k - 1], bc_send.at[idx - 2], bc_recv.at[idx - 2],
-                      {"comp": q // y_size, "row": (q % y_size) * CORES + c})
+        return remote(bc_src.at[idx], bc_buf.at[idx, k], bc_send.at[idx - 2], bc_recv.at[idx - 2],
+                      {"comp": q // y_size, "row": (q % y_size) * CORES + (1 - c)})
 
     def post(idx):
-        return same(half(tot_buf.at[idx], c), post_send.at[idx - 2], post_recv.at[idx - 2], sib)
+        return same(half(tot_buf.at[idx], 1 - c), post_send.at[idx - 2], post_recv.at[idx - 2], sib)
 
     def p2(idx):
         pre(idx).wait()
         bc_src[idx] = lse2_parts([l_buf[idx % 2, pl.ds(2 * c, 2)], pre_buf[idx]])
-        for k in range(1, n_chips):
-            bcast(idx, k).start()
+        for j in range(1, n_chips + 1):
+            bcast(idx, j).start()
 
     def p3(idx):
         same(bc_buf.at[idx], bc_send.at[idx - 2], bc_recv.at[idx - 2], sib).wait()
-        tot_buf[idx, pl.ds(2 * c, 2)] = lse2_parts([bc_src[idx]] + [bc_buf[idx, k] for k in range(n_chips - 1)])
+        tot_buf[idx, pl.ds(2 * (1 - c), 2)] = lse2_parts([bc_buf[idx, k] for k in range(n_chips)])
         post(idx).start()
 
     def zl(s, k):
@@ -321,7 +322,7 @@
 
             @pl.when(jnp.logical_and(s == 0, p == 0))
             def _():
-                pl.semaphore_wait(near_sem, 2 + n_z)
+                pl.semaphore_wait(near_sem, 3 + n_z)
                 signal_z(far_sem)
 
             @pl.when(s == 1)
@@ -545,7 +546,7 @@
             vm((2, comp_size - 1, bt, TP), f32),
             vm((ni, 2, bt, TP), f32),
             vm((ni, 2, bt, TP), f32),
-            vm((ni, n_chips - 1, 2, bt, TP), f32),
+            vm((ni, n_chips, 2, bt, TP), f32),
             vm((ni, row_size, bt, TP), f32),
             dma((6,)), pltpu.SemaphoreType.REGULAR, pltpu.SemaphoreType.REGULAR,
             dma((1,)), dma((2 * ND,)), dma((2 * ND,)), dma((2,)), dma((2,)), dma((2,)),

time: 46.2 us -> 45.8 us (level)
  no operation moved by 1% of the time
where the time goes in v9:
time: 45.8 us; the launch traced here: 45.7 us
  Pallas kernels  45 us (98%)
  between operations  0.64 us (1%)
    pallas_call x1, Pallas kernels, local_fit(): pl.pallas_call(functools.partial(em_kernel, comp_size, row_size, sweeps),...  43.7 us
    pallas_call x1, Pallas kernels, local_fit(): pl.pallas_call(write_kernel, out_shape=tuple((jax.ShapeDtypeStruct(o.shap...  1.35 us

profile of v9, /device:TPU:0, one launch (start us, length us, event | category | flops | bytes accessed | tf_op | source)
XLA Modules:
  0.0 45.7 jit_solution(2266368119473896631)
XLA Ops:
  0.6 43.7 %shard_map.67 = (f32[2,1024,256]{2,1,0:T(8,128)S(1)}, f32[2,1024]{1,0:T(2,128)S(1)}, f32[2,1024]{1,0:T(2,128)S(1)}) custom-call(f32[3]{0:T(128)} %temp_hbm.1, f32[2,1024]{1,0:T(2,128)} %lp_hbm.1, bf16[1024,512]{1,0:T(8,128)(2,1)} %x_hbm.1, f32[2,1024,256]{2,1,0:T(8,128)} %mu_hbm.1), custom_call_target="tpu_custom_call" | custom-call | tf_op jit(solution)/shard_map/pallas_call | solution.py:558
  44.3 1.4 %shard_map.68 = (f32[2,1024,256]{2,1,0:T(8,128)}, f32[2,1024]{1,0:T(2,128)}, f32[2,1024]{1,0:T(2,128)}) custom-call(f32[2,1024,256]{2,1,0:T(8,128)S(1)} %get-tuple-element.6.a, f32[2,1024]{1,0:T(2,128)S(1)} %get-tuple-element.7.b, f32[2,1024]{1,0:T(2,128)S(1)} %get-tuple-element.8.c), custom_call_target="tpu_custom_call" | custom-call | tf_op jit(solution)/shard_map/pallas_call | solution.py:569

commit v10 on v9

--- a/solution.py
+++ b/solution.py
@@ -207,7 +207,7 @@
     def tiles_of(half_id):
         return [(2 * half_id + k // bt, k % bt) for k in range(2 * bt)]
 
-    def e_step(s, t, idx, hook=None):
+    def e_step(s, t, idx, hook=None, early=None):
         def body(i, _):
             h = (1 - c) + i * (2 * c - 1)
             for b, u in tiles_of(h):
@@ -225,6 +225,8 @@
             return 0
 
         lax.fori_loop(0, 2, body, 0)
+        if early is not None:
+            early()
         p2(idx)
 
     def acc_zero():
@@ -381,12 +383,13 @@
         own_out(s).wait_recv()
         acc_zero()
 
-        @pl.when(s == 0)
-        def _():
-            sib_waits(0)
-            y_steps(12, 15)
-
         def body(k, _):
+            @pl.when(jnp.logical_and(s == 0, k == 1))
+            def _():
+                y_steps(12, 14)
+                sib_waits(0)
+                y_steps(14, 15)
+
             @pl.when(jnp.logical_and(s == 1, k == 1))
             def _():
                 z_steps(15, 16)
@@ -394,10 +397,10 @@
 
             mr_half(s, r, 0, y + k * (1 - 2 * y))
 
-            @pl.when(s == 0)
-            def _():
-                y_steps(16 - k, 16)
-                z_steps(8 + 3 * k, 11 + k)
+            @pl.when(jnp.logical_and(s == 0, k == 1))
+            def _():
+                y_steps(15, 16)
+                z_steps(8, 12)
 
             return 0
 
@@ -408,13 +411,18 @@
         def hook(i):
             @pl.when(jnp.logical_and(s == 0, i == 0))
             def _():
-                z_steps(12, 14)
-
-        e_step(s, 1, 2 + s, hook)
+                z_steps(12, 13)
+
+        def first_p3():
+            @pl.when(s == 1)
+            def _():
+                p3(2)
+
+        e_step(s, 1, 2 + s, hook, first_p3)
 
         @pl.when(s == 0)
         def _():
-            z_steps(14, 15)
+            z_steps(13, 15)
 
         return 0
 
@@ -438,7 +446,6 @@
     def sweep(i, _):
         t, s = i // 2, i % 2
         last = t == sweeps - 1
-        p3(i)
         m_step(s, t)
         mean, logw = acc_result()
 
@@ -450,7 +457,7 @@
             def _():
                 brow[s, r] = col_to_row(col)
 
-            e_step(s, t + 1, i + 2)
+            e_step(s, t + 1, i + 2, early=lambda: p3(i + 1))
 
             @pl.when(t == sweeps - 2)
             def _():
@@ -472,6 +479,10 @@
             mean_rows(ry, s)[...] = mean2
             lp_fin[ry, pl.ds(s, 1), :] = col_to_row(logw2)
             fin(ry, s, 1).start()
+
+            @pl.when(s == 0)
+            def _():
+                p3(i + 1)
 
         return 0
 

time: 45.8 us -> 45.8 us (level)
  no operation moved by 1% of the time
where the time goes in v10:
time: 45.8 us; the launch traced here: 45.6 us
  Pallas kernels  45 us (98%)
  between operations  0.64 us (1%)
    pallas_call x1, Pallas kernels, local_fit(): pl.pallas_call(functools.partial(em_kernel, comp_size, row_size, sweeps),...  43.6 us
    pallas_call x1, Pallas kernels, local_fit(): pl.pallas_call(write_kernel, out_shape=tuple((jax.ShapeDtypeStruct(o.shap...  1.35 us

profile of v10, /device:TPU:0, one launch (start us, length us, event | category | flops | bytes accessed | tf_op | source)
XLA Modules:
  0.0 45.6 jit_solution(5442020646759350536)
XLA Ops:
  0.6 43.6 %shard_map.67 = (f32[2,1024,256]{2,1,0:T(8,128)S(1)}, f32[2,1024]{1,0:T(2,128)S(1)}, f32[2,1024]{1,0:T(2,128)S(1)}) custom-call(f32[3]{0:T(128)} %temp_hbm.1, f32[2,1024]{1,0:T(2,128)} %lp_hbm.1, bf16[1024,512]{1,0:T(8,128)(2,1)} %x_hbm.1, f32[2,1024,256]{2,1,0:T(8,128)} %mu_hbm.1), custom_call_target="tpu_custom_call" | custom-call | tf_op jit(solution)/shard_map/pallas_call | solution.py:569
  44.3 1.4 %shard_map.68 = (f32[2,1024,256]{2,1,0:T(8,128)}, f32[2,1024]{1,0:T(2,128)}, f32[2,1024]{1,0:T(2,128)}) custom-call(f32[2,1024,256]{2,1,0:T(8,128)S(1)} %get-tuple-element.6.a, f32[2,1024]{1,0:T(2,128)S(1)} %get-tuple-element.7.b, f32[2,1024]{1,0:T(2,128)S(1)} %get-tuple-element.8.c), custom_call_target="tpu_custom_call" | custom-call | tf_op jit(solution)/shard_map/pallas_call | solution.py:580

commit v11 on v10

--- a/solution.py
+++ b/solution.py
@@ -16,7 +16,8 @@
 CORES = 2
 TP = 256
 NCK = 16
-ND = 8
+ND = 9
+NR = NCK - ND
 
 
 def lse2_parts(parts):
@@ -137,14 +138,14 @@
     def y_out(j):
         return same(xrows(j // ND, r, cid_y(j % ND)), g_send.at[0], y_recv.at[j], yd)
 
-    def z_fwd(j):
-        return same(xrows(j // ND, rx, cid_y(j % ND)), g_send.at[0], z_recv.at[j], zx)
+    def z_fwd(m):
+        return same(xrows(m // NR, rx, cid_y(m % NR)), g_send.at[0], z_recv.at[m], zx)
 
     def sy_fwd(j):
         return same(xrows(j // ND, rx, cid_y(j % ND)), g_send.at[0], sy_recv.at[j // ND], sib)
 
-    def sz_fwd(j):
-        return same(xrows(j // ND, ry, cid_z(j % ND)), g_send.at[0], sz_recv.at[j // ND], sib)
+    def sz_fwd(m):
+        return same(xrows(m // NR, ry, cid_z(m % NR)), g_send.at[0], sz_recv.at[m // NR], sib)
 
     def own_out(s):
         return same(xg.at[s, pl.ds(r * block, block), :], g_send.at[0], own_recv.at[s], sib)
@@ -152,30 +153,34 @@
     def y_steps(a, b):
         def body(j, _):
             y_out(j).wait_recv()
-            z_fwd(j).start()
+
+            @pl.when(j % ND < NR)
+            def _():
+                z_fwd(j // ND * NR + j % ND).start()
+
             sy_fwd(j).start()
             return 0
 
         lax.fori_loop(a, b, body, 0)
 
     def z_steps(a, b):
-        def body(j, _):
-            z_fwd(j).wait_recv()
-            sz_fwd(j).start()
+        def body(m, _):
+            z_fwd(m).wait_recv()
+            sz_fwd(m).start()
             return 0
 
         lax.fori_loop(a, b, body, 0)
 
-    def half_rows(s):
-        return xg.at[s, pl.ds(0, ND * ch), :]
+    def rows_of(s, chunks):
+        return xg.at[s, pl.ds(0, chunks * ch), :]
 
     def sib_waits(s):
-        same(half_rows(s), g_send.at[0], sy_recv.at[s], sib).wait_recv()
-        same(half_rows(s), g_send.at[0], sz_recv.at[s], sib).wait_recv()
+        same(rows_of(s, ND), g_send.at[0], sy_recv.at[s], sib).wait_recv()
+        same(rows_of(s, NR), g_send.at[0], sz_recv.at[s], sib).wait_recv()
 
     def gather_sends_wait(s):
-        for _ in range(4):
-            same(half_rows(s), g_send.at[0], sy_recv.at[s], sib).wait_send()
+        for chunks in (ND, NR, ND, NR):
+            same(rows_of(s, chunks), g_send.at[0], sy_recv.at[s], sib).wait_send()
         own_out(s).wait_send()
 
     x_loads[0].wait()
@@ -372,11 +377,13 @@
     y_steps(6, 8)
     z_steps(0, 4)
     y_steps(8, 9)
-    z_steps(4, 6)
+    z_steps(4, 5)
     y_steps(9, 10)
+    z_steps(5, 6)
     comb(1)
-    z_steps(6, 8)
-    y_steps(10, 12)
+    y_steps(10, 11)
+    z_steps(6, 7)
+    y_steps(11, 12)
 
     def sweep0(s, _):
         same(tot_buf.at[s, pl.ds(0, 3)], ag_send.at[s], ag_recv.at[s], sib).wait()
@@ -392,7 +399,7 @@
 
             @pl.when(jnp.logical_and(s == 1, k == 1))
             def _():
-                z_steps(15, 16)
+                z_steps(12, 14)
                 sib_waits(1)
 
             mr_half(s, r, 0, y + k * (1 - 2 * y))
@@ -400,7 +407,7 @@
             @pl.when(jnp.logical_and(s == 0, k == 1))
             def _():
                 y_steps(15, 16)
-                z_steps(8, 12)
+                z_steps(7, 10)
 
             return 0
 
@@ -411,7 +418,7 @@
         def hook(i):
             @pl.when(jnp.logical_and(s == 0, i == 0))
             def _():
-                z_steps(12, 13)
+                y_steps(16, 17)
 
         def first_p3():
             @pl.when(s == 1)
@@ -422,7 +429,8 @@
 
         @pl.when(s == 0)
         def _():
-            z_steps(13, 15)
+            y_steps(17, 18)
+            z_steps(10, 12)
 
         return 0
 
@@ -560,7 +568,7 @@
             vm((ni, n_chips, 2, bt, TP), f32),
             vm((ni, row_size, bt, TP), f32),
             dma((6,)), pltpu.SemaphoreType.REGULAR, pltpu.SemaphoreType.REGULAR,
-            dma((1,)), dma((2 * ND,)), dma((2 * ND,)), dma((2,)), dma((2,)), dma((2,)),
+            dma((1,)), dma((2 * ND,)), dma((2 * NR,)), dma((2,)), dma((2,)), dma((2,)),
             dma((2,)), dma((2,)), dma((2,)), dma((2,)),
             dma((ni - 2,)), dma((ni - 2,)), dma((ni - 2,)), dma((ni - 2,)), dma((ni - 2,)), dma((ni - 2,)),
             dma((2,)), dma((2,)), dma((2,)), dma((2,)),

time: 45.8 us -> 45.2 us (0.987)
  Pallas kernels: 45 us -> 44.4 us
    pallas_call x1, Pallas kernels: 43.6 us -> 43.1 us  [local_fit(): pl.pallas_call(functools.partial(em_kernel, comp_size, row_size, sweeps),...]
where the time goes in v11:
time: 45.2 us; the launch traced here: 45.1 us
  Pallas kernels  44.4 us (98%)
  between operations  0.64 us (1%)
    pallas_call x1, Pallas kernels, local_fit(): pl.pallas_call(functools.partial(em_kernel, comp_size, row_size, sweeps),...  43.1 us
    pallas_call x1, Pallas kernels, local_fit(): pl.pallas_call(write_kernel, out_shape=tuple((jax.ShapeDtypeStruct(o.shap...  1.35 us

profile of v11, /device:TPU:0, one launch (start us, length us, event | category | flops | bytes accessed | tf_op | source)
XLA Modules:
  0.0 45.1 jit_solution(15857435933073170286)
XLA Ops:
  0.6 43.1 %shard_map.67 = (f32[2,1024,256]{2,1,0:T(8,128)S(1)}, f32[2,1024]{1,0:T(2,128)S(1)}, f32[2,1024]{1,0:T(2,128)S(1)}) custom-call(f32[3]{0:T(128)} %temp_hbm.1, f32[2,1024]{1,0:T(2,128)} %lp_hbm.1, bf16[1024,512]{1,0:T(8,128)(2,1)} %x_hbm.1, f32[2,1024,256]{2,1,0:T(8,128)} %mu_hbm.1), custom_call_target="tpu_custom_call" | custom-call | tf_op jit(solution)/shard_map/pallas_call | solution.py:577
  43.7 1.4 %shard_map.68 = (f32[2,1024,256]{2,1,0:T(8,128)}, f32[2,1024]{1,0:T(2,128)}, f32[2,1024]{1,0:T(2,128)}) custom-call(f32[2,1024,256]{2,1,0:T(8,128)S(1)} %get-tuple-element.6.a, f32[2,1024]{1,0:T(2,128)S(1)} %get-tuple-element.7.b, f32[2,1024]{1,0:T(2,128)S(1)} %get-tuple-element.8.c), custom_call_target="tpu_custom_call" | custom-call | tf_op jit(solution)/shard_map/pallas_call | solution.py:588

commit v12 on v11

--- a/solution.py
+++ b/solution.py
@@ -16,7 +16,7 @@
 CORES = 2
 TP = 256
 NCK = 16
-ND = 9
+ND = 10
 NR = NCK - ND
 
 
@@ -47,7 +47,10 @@
 
 
 def write_kernel(a, b, c, a_out, b_out, c_out, sems):
-    copies = [pltpu.make_async_copy(v, o, sems.at[k]) for k, (v, o) in enumerate(((a, a_out), (b, b_out), (c, c_out)))]
+    n = a.shape[1] // 4
+    pairs = [(a.at[s, pl.ds(q * n, n), :], a_out.at[s, pl.ds(q * n, n), :]) for s in range(2) for q in range(4)]
+    pairs += [(b, b_out), (c, c_out)]
+    copies = [pltpu.make_async_copy(v, o, sems.at[k]) for k, (v, o) in enumerate(pairs)]
     for cp in copies:
         cp.start()
     for cp in copies:
@@ -381,9 +384,7 @@
     y_steps(9, 10)
     z_steps(5, 6)
     comb(1)
-    y_steps(10, 11)
-    z_steps(6, 7)
-    y_steps(11, 12)
+    y_steps(10, 12)
 
     def sweep0(s, _):
         same(tot_buf.at[s, pl.ds(0, 3)], ag_send.at[s], ag_recv.at[s], sib).wait()
@@ -399,7 +400,8 @@
 
             @pl.when(jnp.logical_and(s == 1, k == 1))
             def _():
-                z_steps(12, 14)
+                z_steps(11, 12)
+                y_steps(19, 20)
                 sib_waits(1)
 
             mr_half(s, r, 0, y + k * (1 - 2 * y))
@@ -407,7 +409,7 @@
             @pl.when(jnp.logical_and(s == 0, k == 1))
             def _():
                 y_steps(15, 16)
-                z_steps(7, 10)
+                z_steps(6, 9)
 
             return 0
 
@@ -429,8 +431,8 @@
 
         @pl.when(s == 0)
         def _():
-            y_steps(17, 18)
-            z_steps(10, 12)
+            y_steps(17, 19)
+            z_steps(9, 11)
 
         return 0
 
@@ -590,7 +592,7 @@
             out_shape=tuple(jax.ShapeDtypeStruct(o.shape, o.dtype) for o in outs),
             in_specs=[pl.BlockSpec(memory_space=pltpu.VMEM)] * 3,
             out_specs=(pl.BlockSpec(memory_space=pl.ANY),) * 3,
-            scratch_shapes=[dma((3,))],
+            scratch_shapes=[dma((10,))],
         )(*[pltpu.with_memory_space_constraint(o, pltpu.VMEM) for o in outs])
 
     return jax.shard_map(

time: 45.2 us -> 46.2 us (1.022)
  Pallas kernels: 44.4 us -> 45.4 us
    pallas_call x1, Pallas kernels: 43.1 us -> 44 us  [local_fit(): pl.pallas_call(functools.partial(em_kernel, comp_size, row_size, sweeps),...]
where the time goes in v12:
time: 46.2 us; the launch traced here: 46.1 us
  Pallas kernels  45.4 us (98%)
  between operations  0.64 us (1%)
    pallas_call x1, Pallas kernels, local_fit(): pl.pallas_call(functools.partial(em_kernel, comp_size, row_size, sweeps),...  44 us
    pallas_call x1, Pallas kernels, local_fit(): pl.pallas_call(write_kernel, out_shape=tuple((jax.ShapeDtypeStruct(o.shap...  1.4 us

profile of v12, /device:TPU:0, one launch (start us, length us, event | category | flops | bytes accessed | tf_op | source)
XLA Modules:
  0.0 46.1 jit_solution(15604345796302196833)
XLA Ops:
  0.6 44.0 %shard_map.67 = (f32[2,1024,256]{2,1,0:T(8,128)S(1)}, f32[2,1024]{1,0:T(2,128)S(1)}, f32[2,1024]{1,0:T(2,128)S(1)}) custom-call(f32[3]{0:T(128)} %temp_hbm.1, f32[2,1024]{1,0:T(2,128)} %lp_hbm.1, bf16[1024,512]{1,0:T(8,128)(2,1)} %x_hbm.1, f32[2,1024,256]{2,1,0:T(8,128)} %mu_hbm.1), custom_call_target="tpu_custom_call" | custom-call | tf_op jit(solution)/shard_map/pallas_call | solution.py:579
  44.7 1.4 %shard_map.68 = (f32[2,1024,256]{2,1,0:T(8,128)}, f32[2,1024]{1,0:T(2,128)}, f32[2,1024]{1,0:T(2,128)}) custom-call(f32[2,1024,256]{2,1,0:T(8,128)S(1)} %get-tuple-element.6.a, f32[2,1024]{1,0:T(2,128)S(1)} %get-tuple-element.7.b, f32[2,1024]{1,0:T(2,128)S(1)} %get-tuple-element.8.c), custom_call_target="tpu_custom_call" | custom-call | tf_op jit(solution)/shard_map/pallas_call | solution.py:590

commit v13 on v11

--- a/solution.py
+++ b/solution.py
@@ -230,9 +230,9 @@
             return 0
 
         lax.fori_loop(0, 2, body, 0)
+        p2(idx)
         if early is not None:
             early()
-        p2(idx)
 
     def acc_zero():
         s_acc[...] = jnp.zeros_like(s_acc)

time: 45.2 us -> 44.6 us (0.987)
  Pallas kernels: 44.4 us -> 43.8 us
    pallas_call x1, Pallas kernels: 43.1 us -> 42.5 us  [local_fit(): pl.pallas_call(functools.partial(em_kernel, comp_size, row_size, sweeps),...]
where the time goes in v13:
time: 44.6 us; the launch traced here: 44.5 us
  Pallas kernels  43.8 us (98%)
  between operations  0.64 us (1%)
    pallas_call x1, Pallas kernels, local_fit(): pl.pallas_call(functools.partial(em_kernel, comp_size, row_size, sweeps),...  42.5 us
    pallas_call x1, Pallas kernels, local_fit(): pl.pallas_call(write_kernel, out_shape=tuple((jax.ShapeDtypeStruct(o.shap...  1.35 us

profile of v13, /device:TPU:0, one launch (start us, length us, event | category | flops | bytes accessed | tf_op | source)
XLA Modules:
  0.0 44.5 jit_solution(833768046682409568)
XLA Ops:
  0.6 42.5 %shard_map.67 = (f32[2,1024,256]{2,1,0:T(8,128)S(1)}, f32[2,1024]{1,0:T(2,128)S(1)}, f32[2,1024]{1,0:T(2,128)S(1)}) custom-call(f32[3]{0:T(128)} %temp_hbm.1, f32[2,1024]{1,0:T(2,128)} %lp_hbm.1, bf16[1024,512]{1,0:T(8,128)(2,1)} %x_hbm.1, f32[2,1024,256]{2,1,0:T(8,128)} %mu_hbm.1), custom_call_target="tpu_custom_call" | custom-call | tf_op jit(solution)/shard_map/pallas_call | solution.py:577
  43.1 1.4 %shard_map.68 = (f32[2,1024,256]{2,1,0:T(8,128)}, f32[2,1024]{1,0:T(2,128)}, f32[2,1024]{1,0:T(2,128)}) custom-call(f32[2,1024,256]{2,1,0:T(8,128)S(1)} %get-tuple-element.6.a, f32[2,1024]{1,0:T(2,128)S(1)} %get-tuple-element.7.b, f32[2,1024]{1,0:T(2,128)S(1)} %get-tuple-element.8.c), custom_call_target="tpu_custom_call" | custom-call | tf_op jit(solution)/shard_map/pallas_call | solution.py:588

commit v14 on v13

--- a/solution.py
+++ b/solution.py
@@ -61,9 +61,7 @@
     temp_ref, lp_ref, xg, mu_all, mub, bcol, brow, e_buf, m_buf, l_buf, lq_buf, s_acc, n_acc, lp_fin, sq_buf,
     zl_src, zl_buf, pre_buf, bc_src, bc_buf, tot_buf,
     load_sem, near_sem, far_sem, g_send, y_recv, z_recv, sy_recv, sz_recv, own_recv,
-    zl_send, zl_recv, ag_send, ag_recv,
-    pre_send, pre_recv, bc_send, bc_recv, post_send, post_recv,
-    mx_send, mx_recv, br_send, br_recv, fin_send, fin_recv, lpf_send, lpf_recv,
+    l_send, zl_recv, ag_recv, pre_send, pre_recv, bc_recv, post_recv, mx_recv, br_recv, fin_recv, lpf_recv,
 ):
     z = lax.axis_index("comp")
     r = lax.axis_index("row")
@@ -254,7 +252,7 @@
         def body(i, _):
             @pl.when(i == 1)
             def _():
-                post(idx).wait()
+                post(idx).wait_recv()
 
             def resp_of(b, u):
                 f = jnp.exp2(m_buf[s, b, u:u + 1, :] - tot_buf[idx, b, u:u + 1, :])
@@ -293,11 +291,11 @@
     def bcast(idx, j):
         k = lax.rem(jnp.where(z < comp_size // 2, n_chips - j, j), n_chips)
         q = lax.rem(chip + k, n_chips)
-        return remote(bc_src.at[idx], bc_buf.at[idx, k], bc_send.at[idx - 2], bc_recv.at[idx - 2],
+        return remote(bc_src.at[idx], bc_buf.at[idx, k], l_send.at[0], bc_recv.at[idx - 2],
                       {"comp": q // y_size, "row": (q % y_size) * CORES + (1 - c)})
 
     def post(idx):
-        return same(half(tot_buf.at[idx], 1 - c), post_send.at[idx - 2], post_recv.at[idx - 2], sib)
+        return same(half(tot_buf.at[idx], 1 - c), l_send.at[0], post_recv.at[idx - 2], sib)
 
     def p2(idx):
         pre(idx).wait()
@@ -306,16 +304,16 @@
             bcast(idx, j).start()
 
     def p3(idx):
-        same(bc_buf.at[idx], bc_send.at[idx - 2], bc_recv.at[idx - 2], sib).wait()
+        same(bc_buf.at[idx], l_send.at[0], bc_recv.at[idx - 2], sib).wait_recv()
         tot_buf[idx, pl.ds(2 * (1 - c), 2)] = lse2_parts([bc_buf[idx, k] for k in range(n_chips)])
         post(idx).start()
 
     def zl(s, k):
-        return remote(zl_src.at[s], zl_buf.at[s, k - 1], zl_send.at[s], zl_recv.at[s],
+        return remote(zl_src.at[s], zl_buf.at[s, k - 1], l_send.at[0], zl_recv.at[s],
                       {"comp": lax.rem(z + k, comp_size)})
 
     def ag(s, k):
-        return same(tot_buf.at[s, r], ag_send.at[s], ag_recv.at[s], (sib, yn, yd)[k])
+        return same(tot_buf.at[s, r], l_send.at[0], ag_recv.at[s], (sib, yn, yd)[k])
 
     def orig_fit(s, _):
         def orig_slots(p, _):
@@ -364,7 +362,7 @@
         lax.fori_loop(a, b, send, 0)
 
     def comb(s):
-        same(zl_buf.at[s], zl_send.at[s], zl_recv.at[s], sib).wait()
+        same(zl_buf.at[s], l_send.at[0], zl_recv.at[s], sib).wait_recv()
         tot_buf[s, r] = lse2_parts([zl_src[s]] + [zl_buf[s, k] for k in range(comp_size - 1)])
         for k in range(3):
             ag(s, k).start()
@@ -386,7 +384,7 @@
     y_steps(11, 12)
 
     def sweep0(s, _):
-        same(tot_buf.at[s, pl.ds(0, 3)], ag_send.at[s], ag_recv.at[s], sib).wait()
+        same(tot_buf.at[s, pl.ds(0, 3)], l_send.at[0], ag_recv.at[s], sib).wait_recv()
         own_out(s).wait_recv()
         acc_zero()
 
@@ -437,19 +435,19 @@
     lax.fori_loop(0, 2, sweep0, 0)
 
     def mx(s):
-        return same(mub.at[s, r], mx_send.at[s], mx_recv.at[s], yn)
+        return same(mub.at[s, r], l_send.at[0], mx_recv.at[s], yn)
 
     def br(s):
-        return same(brow.at[s, r], br_send.at[s], br_recv.at[s], yn)
+        return same(brow.at[s, r], l_send.at[0], br_recv.at[s], yn)
 
     def mean_rows(slot, s):
         return mu_out.at[s, pl.ds(pl.multiple_of(slot * n_own, n_own), n_own), :]
 
     def fin(slot, s, k):
-        return same(mean_rows(slot, s), fin_send.at[s, k], fin_recv.at[s, k], sib)
+        return same(mean_rows(slot, s), l_send.at[0], fin_recv.at[s, k], sib)
 
     def lpf(slot, k):
-        return same(lp_fin.at[slot], lpf_send.at[k], lpf_recv.at[k], sib)
+        return same(lp_fin.at[slot], l_send.at[0], lpf_recv.at[k], sib)
 
     def sweep(i, _):
         t, s = i // 2, i % 2
@@ -465,20 +463,23 @@
             def _():
                 brow[s, r] = col_to_row(col)
 
-            e_step(s, t + 1, i + 2, early=lambda: p3(i + 1))
-
-            @pl.when(t == sweeps - 2)
-            def _():
-                mx(s).start()
-                br(s).start()
+            def early():
+                @pl.when(t == sweeps - 2)
+                def _():
+                    mx(s).start()
+                    br(s).start()
+
+                p3(i + 1)
+
+            e_step(s, t + 1, i + 2, early=early)
 
         @pl.when(last)
         def _():
             mean_rows(r, s)[...] = mean
             lp_fin[r, pl.ds(s, 1), :] = col_to_row(logw)
             fin(r, s, 0).start()
-            mx(s).wait()
-            br(s).wait()
+            mx(s).wait_recv()
+            br(s).wait_recv()
             bcol[s, ry] = jnp.broadcast_to(row_to_col(brow[s, ry]), (n_own, 128))
             acc_zero()
 
@@ -512,6 +513,14 @@
     lax.fori_loop(0, 2, sq_norms, 0)
     for s in range(2):
         gather_sends_wait(s)
+        same(zl_buf.at[s], l_send.at[0], zl_recv.at[s], sib).wait_send()
+        same(tot_buf.at[s, pl.ds(0, 3)], l_send.at[0], ag_recv.at[s], sib).wait_send()
+        mx(s).wait_send()
+        br(s).wait_send()
+        for t in range(1, sweeps):
+            same(bc_buf.at[2 * t + s], l_send.at[0], zl_recv.at[s], sib).wait_send()
+            post(2 * t + s).wait_send()
+
 
     t = sweeps - 1
     for s in range(2):
@@ -521,9 +530,13 @@
 
     for k in range(2):
         for s in range(2):
-            fin((r, ry)[k], s, k).wait()
-    lpf(r, 0).wait()
-    lpf(ry, 1).wait()
+            fin((r, ry)[k], s, k).wait_recv()
+    lpf(r, 0).wait_recv()
+    lpf(ry, 1).wait_recv()
+    for k in range(2):
+        for s in range(2):
+            fin((r, ry)[k], s, k).wait_send()
+        lpf((r, ry)[k], k).wait_send()
     for q in range(row_size):
         lp_out[:, q * n_own:(q + 1) * n_own] = lp_fin[q]
 
@@ -569,10 +582,8 @@
             vm((ni, row_size, bt, TP), f32),
             dma((6,)), pltpu.SemaphoreType.REGULAR, pltpu.SemaphoreType.REGULAR,
             dma((1,)), dma((2 * ND,)), dma((2 * NR,)), dma((2,)), dma((2,)), dma((2,)),
-            dma((2,)), dma((2,)), dma((2,)), dma((2,)),
-            dma((ni - 2,)), dma((ni - 2,)), dma((ni - 2,)), dma((ni - 2,)), dma((ni - 2,)), dma((ni - 2,)),
-            dma((2,)), dma((2,)), dma((2,)), dma((2,)),
-            dma((2, 2)), dma((2, 2)), dma((2,)), dma((2,)),
+            dma((1,)), dma((2,)), dma((2,)), dma((ni - 2,)), dma((ni - 2,)), dma((ni - 2,)), dma((ni - 2,)),
+            dma((2,)), dma((2,)), dma((2, 2)), dma((2,)),
         ]
         outs = pl.pallas_call(
             functools.partial(em_kernel, comp_size, row_size, sweeps),

time: 44.6 us -> 44.3 us (level)
  no operation moved by 1% of the time
where the time goes in v14:
time: 44.3 us; the launch traced here: 44.1 us
  Pallas kernels  43.5 us (98%)
  between operations  0.64 us (1%)
    pallas_call x1, Pallas kernels, local_fit(): pl.pallas_call(functools.partial(em_kernel, comp_size, row_size, sweeps),...  42.1 us
    pallas_call x1, Pallas kernels, local_fit(): pl.pallas_call(write_kernel, out_shape=tuple((jax.ShapeDtypeStruct(o.shap...  1.35 us

profile of v14, /device:TPU:0, one launch (start us, length us, event | category | flops | bytes accessed | tf_op | source)
XLA Modules:
  0.0 44.1 jit_solution(6417276738623295849)
XLA Ops:
  0.6 42.1 %shard_map.67 = (f32[2,1024,256]{2,1,0:T(8,128)S(1)}, f32[2,1024]{1,0:T(2,128)S(1)}, f32[2,1024]{1,0:T(2,128)S(1)}) custom-call(f32[3]{0:T(128)} %temp_hbm.1, f32[2,1024]{1,0:T(2,128)} %lp_hbm.1, bf16[1024,512]{1,0:T(8,128)(2,1)} %x_hbm.1, f32[2,1024,256]{2,1,0:T(8,128)} %mu_hbm.1), custom_call_target="tpu_custom_call" | custom-call | tf_op jit(solution)/shard_map/pallas_call | solution.py:588
  42.7 1.4 %shard_map.68 = (f32[2,1024,256]{2,1,0:T(8,128)}, f32[2,1024]{1,0:T(2,128)}, f32[2,1024]{1,0:T(2,128)}) custom-call(f32[2,1024,256]{2,1,0:T(8,128)S(1)} %get-tuple-element.6.a, f32[2,1024]{1,0:T(2,128)S(1)} %get-tuple-element.7.b, f32[2,1024]{1,0:T(2,128)S(1)} %get-tuple-element.8.c), custom_call_target="tpu_custom_call" | custom-call | tf_op jit(solution)/shard_map/pallas_call | solution.py:599

commit v15 on v14

--- a/solution.py
+++ b/solution.py
@@ -393,18 +393,17 @@
             def _():
                 y_steps(12, 14)
                 sib_waits(0)
-                y_steps(14, 15)
 
             @pl.when(jnp.logical_and(s == 1, k == 1))
             def _():
-                z_steps(12, 14)
+                z_steps(13, 14)
                 sib_waits(1)
 
             mr_half(s, r, 0, y + k * (1 - 2 * y))
 
             @pl.when(jnp.logical_and(s == 0, k == 1))
             def _():
-                y_steps(15, 16)
+                y_steps(14, 16)
                 z_steps(7, 10)
 
             return 0
@@ -428,7 +427,7 @@
         @pl.when(s == 0)
         def _():
             y_steps(17, 18)
-            z_steps(10, 12)
+            z_steps(10, 13)
 
         return 0
 

time: 44.3 us -> 44 us (level)
  no operation moved by 1% of the time
where the time goes in v15:
time: 44 us; the launch traced here: 43.9 us
  Pallas kernels  43.2 us (98%)
  between operations  0.64 us (1%)
    pallas_call x1, Pallas kernels, local_fit(): pl.pallas_call(functools.partial(em_kernel, comp_size, row_size, sweeps),...  41.9 us
    pallas_call x1, Pallas kernels, local_fit(): pl.pallas_call(write_kernel, out_shape=tuple((jax.ShapeDtypeStruct(o.shap...  1.35 us

profile of v15, /device:TPU:0, one launch (start us, length us, event | category | flops | bytes accessed | tf_op | source)
XLA Modules:
  0.0 43.9 jit_solution(150493090492854847)
XLA Ops:
  0.6 41.9 %shard_map.67 = (f32[2,1024,256]{2,1,0:T(8,128)S(1)}, f32[2,1024]{1,0:T(2,128)S(1)}, f32[2,1024]{1,0:T(2,128)S(1)}) custom-call(f32[3]{0:T(128)} %temp_hbm.1, f32[2,1024]{1,0:T(2,128)} %lp_hbm.1, bf16[1024,512]{1,0:T(8,128)(2,1)} %x_hbm.1, f32[2,1024,256]{2,1,0:T(8,128)} %mu_hbm.1), custom_call_target="tpu_custom_call" | custom-call | tf_op jit(solution)/shard_map/pallas_call | solution.py:587
  42.5 1.4 %shard_map.68 = (f32[2,1024,256]{2,1,0:T(8,128)}, f32[2,1024]{1,0:T(2,128)}, f32[2,1024]{1,0:T(2,128)}) custom-call(f32[2,1024,256]{2,1,0:T(8,128)S(1)} %get-tuple-element.6.a, f32[2,1024]{1,0:T(2,128)S(1)} %get-tuple-element.7.b, f32[2,1024]{1,0:T(2,128)S(1)} %get-tuple-element.8.c), custom_call_target="tpu_custom_call" | custom-call | tf_op jit(solution)/shard_map/pallas_call | solution.py:598

commit v16 on v15

--- a/solution.py
+++ b/solution.py
@@ -456,16 +456,13 @@
 
         @pl.when(t < sweeps - 1)
         def _():
-            col = set_params(s, r, mean, logw, t + 1)
-
-            @pl.when(t == sweeps - 2)
-            def _():
-                brow[s, r] = col_to_row(col)
+            set_params(s, r, mean, logw, t + 1)
 
             def early():
                 @pl.when(t == sweeps - 2)
                 def _():
                     mx(s).start()
+                    brow[s, r] = col_to_row(bcol[s, r][:, :1])
                     br(s).start()
 
                 p3(i + 1)
@@ -475,8 +472,8 @@
         @pl.when(last)
         def _():
             mean_rows(r, s)[...] = mean
+            fin(r, s, 0).start()
             lp_fin[r, pl.ds(s, 1), :] = col_to_row(logw)
-            fin(r, s, 0).start()
             mx(s).wait_recv()
             br(s).wait_recv()
             bcol[s, ry] = jnp.broadcast_to(row_to_col(brow[s, ry]), (n_own, 128))
@@ -485,8 +482,8 @@
             mr_all(s, ry, t)
             mean2, logw2 = acc_result()
             mean_rows(ry, s)[...] = mean2
+            fin(ry, s, 1).start()
             lp_fin[ry, pl.ds(s, 1), :] = col_to_row(logw2)
-            fin(ry, s, 1).start()
 
             @pl.when(s == 0)
             def _():

time: 44 us -> 44 us (level)
  no operation moved by 1% of the time
where the time goes in v16:
time: 44 us; the launch traced here: 43.8 us
  Pallas kernels  43.2 us (98%)
  between operations  0.64 us (1%)
    pallas_call x1, Pallas kernels, local_fit(): pl.pallas_call(functools.partial(em_kernel, comp_size, row_size, sweeps),...  41.8 us
    pallas_call x1, Pallas kernels, local_fit(): pl.pallas_call(write_kernel, out_shape=tuple((jax.ShapeDtypeStruct(o.shap...  1.35 us

profile of v16, /device:TPU:0, one launch (start us, length us, event | category | flops | bytes accessed | tf_op | source)
XLA Modules:
  0.0 43.8 jit_solution(3381355300107479769)
XLA Ops:
  0.6 41.8 %shard_map.67 = (f32[2,1024,256]{2,1,0:T(8,128)S(1)}, f32[2,1024]{1,0:T(2,128)S(1)}, f32[2,1024]{1,0:T(2,128)S(1)}) custom-call(f32[3]{0:T(128)} %temp_hbm.1, f32[2,1024]{1,0:T(2,128)} %lp_hbm.1, bf16[1024,512]{1,0:T(8,128)(2,1)} %x_hbm.1, f32[2,1024,256]{2,1,0:T(8,128)} %mu_hbm.1), custom_call_target="tpu_custom_call" | custom-call | tf_op jit(solution)/shard_map/pallas_call | solution.py:584
  42.5 1.4 %shard_map.68 = (f32[2,1024,256]{2,1,0:T(8,128)}, f32[2,1024]{1,0:T(2,128)}, f32[2,1024]{1,0:T(2,128)}) custom-call(f32[2,1024,256]{2,1,0:T(8,128)S(1)} %get-tuple-element.6.a, f32[2,1024]{1,0:T(2,128)S(1)} %get-tuple-element.7.b, f32[2,1024]{1,0:T(2,128)S(1)} %get-tuple-element.8.c), custom_call_target="tpu_custom_call" | custom-call | tf_op jit(solution)/shard_map/pallas_call | solution.py:595

commit v17 on v16

--- a/solution.py
+++ b/solution.py
@@ -367,7 +367,7 @@
         for k in range(3):
             ag(s, k).start()
 
-    early = ND + 3
+    early = ND + 4
     y_sends(ND, early)
     y_steps(5, 6)
     comb(0)

time: 44 us -> 44.4 us (level)
  no operation moved by 1% of the time
where the time goes in v17:
time: 44.4 us; the launch traced here: 44.2 us
  Pallas kernels  43.6 us (98%)
  between operations  0.64 us (1%)
    pallas_call x1, Pallas kernels, local_fit(): pl.pallas_call(functools.partial(em_kernel, comp_size, row_size, sweeps),...  42.2 us
    pallas_call x1, Pallas kernels, local_fit(): pl.pallas_call(write_kernel, out_shape=tuple((jax.ShapeDtypeStruct(o.shap...  1.35 us

profile of v17, /device:TPU:0, one launch (start us, length us, event | category | flops | bytes accessed | tf_op | source)
XLA Modules:
  0.0 44.2 jit_solution(17099876455379231531)
XLA Ops:
  0.6 42.2 %shard_map.67 = (f32[2,1024,256]{2,1,0:T(8,128)S(1)}, f32[2,1024]{1,0:T(2,128)S(1)}, f32[2,1024]{1,0:T(2,128)S(1)}) custom-call(f32[3]{0:T(128)} %temp_hbm.1, f32[2,1024]{1,0:T(2,128)} %lp_hbm.1, bf16[1024,512]{1,0:T(8,128)(2,1)} %x_hbm.1, f32[2,1024,256]{2,1,0:T(8,128)} %mu_hbm.1), custom_call_target="tpu_custom_call" | custom-call | tf_op jit(solution)/shard_map/pallas_call | solution.py:584
  42.9 1.4 %shard_map.68 = (f32[2,1024,256]{2,1,0:T(8,128)}, f32[2,1024]{1,0:T(2,128)}, f32[2,1024]{1,0:T(2,128)}) custom-call(f32[2,1024,256]{2,1,0:T(8,128)S(1)} %get-tuple-element.6.a, f32[2,1024]{1,0:T(2,128)S(1)} %get-tuple-element.7.b, f32[2,1024]{1,0:T(2,128)S(1)} %get-tuple-element.8.c), custom_call_target="tpu_custom_call" | custom-call | tf_op jit(solution)/shard_map/pallas_call | solution.py:595
